TPU v7x, 32 devices: a whole 2x2x4 slice. The times are simulated.
32 devices in a mesh: dp: 2 (over core), seq: 4 (over z), tensor: 4 (over y, x).
Axes of the slice: x: 2, y: 2, z: 4, core: 2. Of those that a mesh axis runs over, the one named last changes fastest.
Arguments:
- tokens: bfloat16 [4, 4096, 1024], P('dp', ('seq', 'tensor')), may hold values from -6 to 6
- w_query: bfloat16 [1024, 1024], replicated, may hold values from -0.1875 to 0.1875
- w_key: bfloat16 [1024, 1024], replicated, may hold values from -0.1875 to 0.1875
- w_value: bfloat16 [1024, 1024], replicated, may hold values from -0.1875 to 0.1875
- w_ugate: bfloat16 [1024, 1024], replicated, may hold values from -0.1875 to 0.1875
- w_output: bfloat16 [1024, 1024], replicated, may hold values from -0.1875 to 0.1875
- w_left: bfloat16 [1024, 2816], P(None, 'tensor'), may hold values from -0.1875 to 0.1875
- w_right: bfloat16 [1024, 2816], P(None, 'tensor'), may hold values from -0.1875 to 0.1875
- w_down: bfloat16 [2816, 1024], P('tensor'), may hold values from -0.109375 to 0.109375
- decay_rate: float32 [8], replicated, may hold values from 0.00012207031 to 0.05
- cotangent: bfloat16 [4, 4096, 1024], P('dp', ('seq', 'tensor')), may hold values from -6 to 6
Outputs:
- mixed_out: bfloat16 [4, 4096, 1024], P('dp', ('seq', 'tensor'))
- grad_tokens: float32 [4, 4096, 1024], P('dp', ('seq', 'tensor'))
- grad_query: float32 [1024, 1024], replicated
- grad_key: float32 [1024, 1024], replicated
- grad_value: float32 [1024, 1024], replicated
- grad_ugate: float32 [1024, 1024], replicated
- grad_output: float32 [1024, 1024], replicated
- grad_left: float32 [1024, 2816], P(None, 'tensor')
- grad_right: float32 [1024, 2816], P(None, 'tensor')
- grad_down: float32 [2816, 1024], P('tensor')
All inputs are finite; a program needn't handle non-finite values.
Results may differ from a plain program's by a relative error of at most 0.017.
Values may be sent and summed in bfloat16 or wider, within the bound.
A program may use at most 320 MiB of HBM per device.

v0:
```python
import functools

import jax
import jax.numpy as jnp
from jax import lax
from jax.experimental import pallas as pl
from jax.experimental.pallas import tpu as pltpu
from jax.sharding import PartitionSpec as P


EPS = 1e-06
F32 = jnp.float32
BF16 = jnp.bfloat16


def swap(value, axis, bit):
    count = lax.axis_size(axis)
    return jax.tree.map(
        lambda v: lax.ppermute(v, axis, [(i, i ^ bit) for i in range(count)]), value
    )


CHUNK = 256
LAG = 2


def added(first, second):
    return (first.astype(F32) + second.astype(F32)).astype(BF16)


def reduce_kernel(
    depth,
    grads,
    pair_in,
    out,
    pair_out,
    own,
    core_in,
    first_in,
    second_in,
    line_in,
    line_mid,
    pair_line,
    pair_mid,
    sems,
    pair_sems,
    load_sem,
):
    core = lax.axis_index("dp")
    slot = lax.axis_index("tensor")
    place = lax.axis_index("seq")
    rows = own.shape[0]
    chunks = rows // CHUNK
    half, quarter, eighth = CHUNK // 2, CHUNK // 4, CHUNK // 8
    low_side = place < depth // 2
    outermost = (place == 0) | (place == depth - 1)
    middle = (place == depth // 2 - 1) | (place == depth // 2)
    inward = jnp.where(low_side, place + 1, place - 1)
    outward = jnp.where(low_side, place - 1, place + 1)

    barrier = pltpu.get_barrier_semaphore()

    def greet(peer):
        pl.semaphore_signal(
            barrier, inc=1, device_id=peer, device_id_type=pl.DeviceIdType.MESH
        )

    greet({"dp": 1 - core})
    greet({"tensor": slot ^ 1})
    greet({"tensor": slot ^ 2})

    @pl.when(place > 0)
    def _():
        greet({"seq": place - 1})

    @pl.when(place < depth - 1)
    def _():
        greet({"seq": place + 1})

    pl.semaphore_wait(barrier, jnp.where(outermost, 4, 5))

    def remote(source, target, sem, at, peer):
        return pltpu.make_async_remote_copy(
            src_ref=source,
            dst_ref=target,
            send_sem=sem.at[0, at],
            recv_sem=sem.at[1, at],
            device_id=peer,
            device_id_type=pl.DeviceIdType.MESH,
        )

    def span(start, size):
        return pl.ds(pl.multiple_of(start, size), size)

    def bits(q):
        first = jnp.where(q % 2 == 0, 1, 2)
        second = 3 - first
        return first, second, (slot & first) // first, (slot & second) // second

    def base(q):
        return pl.multiple_of(q * CHUNK, CHUNK)

    def to_core(q):
        return remote(
            own.at[span(base(q) + (1 - core) * half, half)],
            core_in.at[q],
            sems.at[0],
            q,
            {"dp": 1 - core},
        )

    def to_first(q):
        first, _, f, _ = bits(q)
        return remote(
            core_in.at[q, span((1 - f) * quarter, quarter)],
            first_in.at[q],
            sems.at[1],
            q,
            {"tensor": slot ^ first},
        )

    def to_second(q):
        _, second, _, g = bits(q)
        return remote(
            first_in.at[q, span((1 - g) * eighth, eighth)],
            second_in.at[q],
            sems.at[2],
            q,
            {"tensor": slot ^ second},
        )

    def block(q):
        _, _, f, g = bits(q)
        return base(q) + core * half + f * quarter + g * eighth

    def back_second(q):
        _, second, _, _ = bits(q)
        at = span(block(q), eighth)
        return remote(out.at[at], out.at[at], sems.at[3], q, {"tensor": slot ^ second})

    def back_first(q):
        first, _, f, _ = bits(q)
        at = span(base(q) + core * half + f * quarter, quarter)
        return remote(out.at[at], out.at[at], sems.at[4], q, {"tensor": slot ^ first})

    def back_core(q):
        at = span(base(q) + core * half, half)
        return remote(out.at[at], out.at[at], sems.at[5], q, {"dp": 1 - core})

    class Line:
        def __init__(self, mine, came, met, total, sem, offset):
            self.mine, self.came, self.met, self.total = mine, came, met, total
            self.sem, self.offset = sem, offset

        def inwards(self, q, source):
            return remote(
                source, self.came(q), self.sem.at[self.offset], q, {"seq": inward}
            )

        def across(self, q):
            return remote(
                self.came(q),
                self.met(q),
                self.sem.at[self.offset + 1],
                q,
                {"seq": depth - 1 - place},
            )

        def outwards(self, q):
            return remote(
                self.total(q), self.total(q), self.sem.at[self.offset + 2], q, {"seq": outward}
            )

        def step_in(self, q):
            @pl.when(outermost)
            def _():
                self.inwards(q, self.mine(q)).start()

        def step_middle(self, q):
            @pl.when(jnp.logical_not(outermost))
            def _():
                self.inwards(q, self.mine(q)).wait_recv()
                came = self.came(q)
                came[...] = added(self.mine(q)[...], came[...])

                @pl.when(middle)
                def _():
                    self.across(q).start()

                @pl.when(jnp.logical_not(middle))
                def _():
                    self.inwards(q, came).start()

        def step_out(self, q):
            @pl.when(middle)
            def _():
                self.across(q).wait_recv()
                self.total(q)[...] = added(self.came(q)[...], self.met(q)[...])

            @pl.when(jnp.logical_not(outermost))
            def _():
                @pl.when(jnp.logical_not(middle))
                def _():
                    self.outwards(q).wait_recv()

                self.outwards(q).start()

        def step_last(self, q):
            @pl.when(outermost)
            def _():
                self.outwards(q).wait_recv()

        def settle(self, q):
            @pl.when(outermost)
            def _():
                self.inwards(q, self.mine(q)).wait_send()

            @pl.when(jnp.logical_not(outermost))
            def _():
                @pl.when(middle)
                def _():
                    self.across(q).wait_send()

                @pl.when(jnp.logical_not(middle))
                def _():
                    self.inwards(q, self.came(q)).wait_send()

                self.outwards(q).wait_send()

    def second_mine(q):
        return second_in.at[q]

    line = Line(
        second_mine,
        lambda q: line_in.at[q],
        lambda q: line_mid.at[q],
        lambda q: out.at[span(block(q), eighth)],
        sems,
        6,
    )
    pair_chunks, pair_rows, pair_cols = pair_line.shape
    pair = Line(
        lambda q: pair_in.at[span(q * pair_rows, pair_rows)],
        lambda q: pair_line.at[q],
        lambda q: pair_mid.at[q],
        lambda q: pair_out.at[span(q * pair_rows, pair_rows), span(core * pair_cols, pair_cols)],
        pair_sems,
        0,
    )

    def pair_core(q):
        return remote(pair.total(q), pair.total(q), pair_sems.at[3], q, {"dp": 1 - core})

    size = rows // len(grads)
    loads = [
        pltpu.make_async_copy(g, own.at[pl.ds(i * size, size)], load_sem.at[i])
        for i, g in enumerate(grads)
    ]
    for load in loads:
        load.start()
    per_load = size // CHUNK
    for i, load in enumerate(loads):
        load.wait()

        @pl.loop(i * per_load, (i + 1) * per_load)
        def _(q):
            to_core(q).start()

    def stage_a(q):
        to_core(q).wait_recv()
        came = core_in.at[q]
        came[...] = added(own[span(base(q) + core * half, half)], came[...])

    def stage_b(q):
        _, _, f, _ = bits(q)
        to_first(q).wait_recv()
        came = first_in.at[q]
        came[...] = added(core_in[q, span(f * quarter, quarter)], came[...])

    def stage_c(q):
        _, _, _, g = bits(q)
        to_second(q).wait_recv()
        came = second_in.at[q]
        came[...] = added(first_in[q, span(g * eighth, eighth)], came[...])

    pairs = chunks // 2

    def during(step, lag, count, action):
        i = step - lag

        @pl.when((i >= 0) & (i < count))
        def _():
            action(i)

    def both(action):
        def run(i):
            action(2 * i)
            action(2 * i + 1)

        return run

    def start(copy):
        return lambda q: copy(q).start()

    def arrived(copy, following):
        def run(q):
            copy(q).wait_recv()
            following(q).start()

        return run

    def last_then_second(q):
        line.step_last(q)
        back_second(q).start()

    def finish_pair(q):
        pair.step_last(q)
        pair_core(q).start()

    steps = max(pairs + 7 * LAG, pair_chunks + 3 * LAG) + 1

    @pl.loop(0, steps)
    def _(step):
        during(step, 7 * LAG, pairs, both(arrived(back_first, back_core)))
        during(step, 6 * LAG, pairs, both(arrived(back_second, back_first)))
        during(step, 5 * LAG, pairs, both(last_then_second))
        during(step, 4 * LAG, pairs, both(line.step_out))
        during(step, 3 * LAG, pairs, both(line.step_middle))
        during(step, 2 * LAG, pairs, both(stage_c))
        during(step, LAG, pairs, both(stage_b))
        during(step, 0, pairs, both(stage_a))
        during(step, 2 * LAG, pairs, both(line.step_in))
        during(step, LAG, pairs, both(start(to_second)))
        during(step, 0, pairs, both(start(to_first)))
        during(step, 3 * LAG, pair_chunks, finish_pair)
        during(step, 2 * LAG, pair_chunks, pair.step_out)
        during(step, LAG, pair_chunks, pair.step_middle)
        during(step, 0, pair_chunks, pair.step_in)

    @pl.loop(0, chunks)
    def _(q):
        back_core(q).wait_recv()
        for copy in (to_core, to_first, to_second, back_second, back_first, back_core):
            copy(q).wait_send()
        line.settle(q)

    @pl.loop(0, pair_chunks)
    def _(q):
        pair_core(q).wait()
        pair.settle(q)


def reduce_grads(grads, pair_half, depth):
    size, width = grads[0].shape
    rows = size * len(grads)
    chunks = rows // CHUNK
    pair_chunks = 12
    pair_rows, pair_cols = pair_half.shape[0] // pair_chunks, pair_half.shape[1]
    vmem = pl.BlockSpec(memory_space=pltpu.VMEM)

    def body(*refs):
        reduce_kernel(depth, refs[: len(grads)], *refs[len(grads) :])

    return pl.pallas_call(
        body,
        out_shape=(
            jax.ShapeDtypeStruct((rows, width), BF16),
            jax.ShapeDtypeStruct((pair_half.shape[0], 2 * pair_cols), BF16),
        ),
        in_specs=[pl.BlockSpec(memory_space=pl.ANY)] * len(grads) + [vmem],
        out_specs=(vmem, vmem),
        scratch_shapes=[
            pltpu.VMEM((rows, width), BF16),
            pltpu.VMEM((chunks, CHUNK // 2, width), BF16),
            pltpu.VMEM((chunks, CHUNK // 4, width), BF16),
            pltpu.VMEM((chunks, CHUNK // 8, width), BF16),
            pltpu.VMEM((chunks, CHUNK // 8, width), BF16),
            pltpu.VMEM((chunks, CHUNK // 8, width), BF16),
            pltpu.VMEM((pair_chunks, pair_rows, pair_cols), BF16),
            pltpu.VMEM((pair_chunks, pair_rows, pair_cols), BF16),
            pltpu.SemaphoreType.DMA((9, 2, chunks)),
            pltpu.SemaphoreType.DMA((4, 2, pair_chunks)),
            pltpu.SemaphoreType.DMA((len(grads),)),
        ],
        compiler_params=pltpu.CompilerParams(
            collective_id=1, has_side_effects=True, vmem_limit_bytes=60 * 1024 * 1024
        ),
        name="reduce_grads",
    )(*grads, pair_half)


ROWS = 256


def times(x, w):
    return jnp.dot(x, w, preferred_element_type=F32)


def times_back(x, w):
    return lax.dot_general(x, w, (((1,), (1,)), ((), ())), preferred_element_type=F32)


def times_rows(x, y):
    return lax.dot_general(x, y, (((0,), (0,)), ((), ())), preferred_element_type=F32)


def hidden_kernel(rows, grads, left, right, down, other, *rest):
    mixed, back, own_kept, other_kept, acc_mixed, acc_back = rest[-6:]

    def unit(kept, w_left, w_right, w_down):
        e1, e2 = times_back(rows[...], w_left), times_back(rows[...], w_right)
        dm = times_back(grads[...], w_down)
        kept[2] = (e1 * e2).astype(BF16)
        kept[0] = (dm * e2).astype(BF16)
        kept[1] = (dm * e1).astype(BF16)
        return times(kept[2], w_down), times(kept[0], w_left) + times(kept[1], w_right)

    acc_mixed[...], acc_back[...] = unit(own_kept, left[...], right[...], down[...])
    more_mixed, more_back = unit(other_kept, other[0], other[1], other[2])
    mixed[...] = (acc_mixed[...] + more_mixed).astype(mixed.dtype)
    back[...] = (acc_back[...] + more_back).astype(back.dtype)


def hidden_part(rows, grads, weights, kept, out_type):
    count, width = rows.shape
    hidden = weights[0].shape[0]
    first = 0 if kept is None else count // ROWS

    def whole(array):
        return pl.BlockSpec(array.shape, lambda i: (0,) * array.ndim)

    row_spec = pl.BlockSpec((ROWS, width), lambda i: (i, 0))
    kept_spec = pl.BlockSpec((3, ROWS, hidden), lambda i: (0, i + first, 0))
    extra = [] if kept is None else list(kept)
    held = 2 + len(weights)

    def body(*refs):
        hidden_kernel(*refs[:held], *refs[held + len(extra) :])

    outs = pl.pallas_call(
        body,
        grid=(count // ROWS,),
        out_shape=(jax.ShapeDtypeStruct((count, width), out_type),) * 2
        + (jax.ShapeDtypeStruct((3, 2 * count, hidden), BF16),) * 2,
        in_specs=[row_spec, row_spec]
        + [whole(w) for w in weights]
        + [pl.BlockSpec(memory_space=pl.ANY)] * len(extra),
        out_specs=(row_spec, row_spec, kept_spec, kept_spec),
        scratch_shapes=[pltpu.VMEM((ROWS, width), F32), pltpu.VMEM((ROWS, width), F32)],
        input_output_aliases={held + i: 2 + i for i in range(len(extra))},
        compiler_params=pltpu.CompilerParams(vmem_limit_bytes=56 * 1024 * 1024),
        cost_estimate=pl.CostEstimate(
            flops=24 * count * width * hidden,
            bytes_accessed=12 * width * hidden + 12 * count * hidden + 12 * count * width,
            transcendentals=0,
        ),
        name="hidden_part",
    )(rows, grads, *weights, *extra)
    return outs[0], outs[1], outs[2:]


def hidden_grads_kernel(kept, rows_own, rows_nb, grads_own, grads_nb, mine, theirs):
    core = lax.axis_index("dp")
    half = mine.shape[2]
    count = rows_own.shape[0]
    for out, which in ((mine, core), (theirs, 1 - core)):
        at = pl.ds(pl.multiple_of(which * half, half), half)

        @pl.when(pl.program_id(0) < 2)
        def _(out=out, at=at):
            out[0] = (
                times_rows(kept[0, :count], rows_own[:, at])
                + times_rows(kept[0, count:], rows_nb[:, at])
            ).astype(BF16)

        @pl.when(pl.program_id(0) == 2)
        def _(out=out, at=at):
            out[0] = (
                times_rows(kept[0, :count], grads_own[:, at])
                + times_rows(kept[0, count:], grads_nb[:, at])
            ).astype(BF16)


def hidden_grads(kept, rows_own, rows_nb, grads_own, grads_nb):
    count, width = rows_own.shape
    hidden = kept.shape[2]
    whole = pl.BlockSpec((count, width), lambda i: (0, 0))
    out_spec = pl.BlockSpec((1, hidden, width // 2), lambda i: (i, 0, 0))
    return pl.pallas_call(
        hidden_grads_kernel,
        grid=(3,),
        out_shape=(jax.ShapeDtypeStruct((3, hidden, width // 2), BF16),) * 2,
        in_specs=[pl.BlockSpec((1, 2 * count, hidden), lambda i: (i, 0, 0))] + [whole] * 4,
        out_specs=(out_spec, out_spec),
        compiler_params=pltpu.CompilerParams(vmem_limit_bytes=40 * 1024 * 1024),
        cost_estimate=pl.CostEstimate(
            flops=12 * count * width * hidden,
            bytes_accessed=12 * count * hidden + 8 * count * width + 6 * width * hidden,
            transcendentals=0,
        ),
        name="hidden_grads",
    )(kept, rows_own, rows_nb, grads_own, grads_nb)


MESH = pl.DeviceIdType.MESH


class States:
    def __init__(self, depth, width, backward, powers, local, came, total, far, outs, states, sems):
        self.depth, self.width, self.backward, self.powers = depth, width, backward, powers
        self.local, self.came, self.total, self.far = local, came, total, far
        self.outs, self.states, self.sems = outs, states, sems
        self.slot = lax.axis_index("tensor")
        self.place = lax.axis_index("seq")
        self.share = local.shape[0] // width

    def greet(self, more=()):
        barrier = pltpu.get_barrier_semaphore()
        for peer in more:
            pl.semaphore_signal(barrier, inc=1, device_id=peer, device_id_type=MESH)
        for b in range(1, self.width):
            pl.semaphore_signal(
                barrier, inc=1, device_id={"tensor": self.slot ^ b}, device_id_type=MESH
            )
        for j in range(1, self.depth):
            peer = lax.rem(self.place + j, self.depth)
            pl.semaphore_signal(barrier, inc=1, device_id={"seq": peer}, device_id_type=MESH)
        pl.semaphore_wait(barrier, self.width + self.depth - 2 + len(more))

    def copy(self, source, target, at, peer):
        return pltpu.make_async_remote_copy(
            src_ref=source,
            dst_ref=target,
            send_sem=self.sems.at[0, at],
            recv_sem=self.sems.at[1, at],
            device_id=peer,
            device_id_type=MESH,
        )

    def group(self, slot):
        return pl.ds(slot * self.share, self.share)

    def to_peer(self, b):
        peer = self.slot ^ b
        return self.copy(
            self.local.at[self.group(peer)], self.came.at[b - 1], b - 1, {"tensor": peer}
        )

    def to_far(self, j):
        peer = self.place - j if self.backward else self.place + j
        return self.copy(self.total, self.far.at[j - 1], self.width + j - 2, {"seq": peer})

    def has_far(self, j):
        return self.place >= j if self.backward else self.place + j < self.depth

    def from_far(self, j):
        return self.place + j < self.depth if self.backward else self.place >= j

    def to_owner(self, d):
        at = self.width + self.depth - 2 + d - 1
        return self.copy(
            self.outs.at[d - 1],
            self.states.at[self.group(self.slot)],
            at,
            {"tensor": self.slot ^ d},
        )

    def power(self, count, head):
        return self.powers[count, head]

    def piece(self, b, k, s):
        if b == 0:
            return self.local[self.slot * self.share + k, s].astype(F32)
        return self.came[b - 1, k, s].astype(F32)

    def gather(self):
        for b in range(1, self.width):
            self.to_peer(b).wait_recv()
        for k in range(self.share):
            head = self.slot * self.share + k
            for s in range(self.local.shape[1]):
                value = 0.0
                for b in range(self.width):
                    spot = self.slot ^ b
                    left = spot if self.backward else self.width - 1 - spot
                    value = value + self.power(left, head) * self.piece(b, k, s)
                self.total[k, s] = value.astype(BF16)
        for j in range(1, self.depth):

            @pl.when(self.has_far(j))
            def _(j=j):
                self.to_far(j).start()

    def send_back(self, entering):
        for j in range(1, self.depth):

            @pl.when(self.from_far(j))
            def _(j=j):
                self.to_far(j).wait_recv()

            @pl.when(jnp.logical_not(self.from_far(j)))
            def _(j=j):
                self.far[j - 1] = jnp.zeros(self.far.shape[1:], BF16)

        for k in range(self.share):
            head = self.slot * self.share + k
            for s in range(self.local.shape[1]):
                value = 0.0
                for j in range(1, self.depth):
                    value = value + self.power(self.width * (j - 1), head) * self.far[
                        j - 1, k, s
                    ].astype(F32)
                entering[k, s] = value
        for d in list(range(1, self.width)) + [0]:
            target = self.slot ^ d
            inner = self.width - 1 - target if self.backward else target
            for k in range(self.share):
                head = self.slot * self.share + k
                for s in range(self.local.shape[1]):
                    value = self.power(inner, head) * entering[k, s]
                    for b in range(self.width):
                        if b == d:
                            continue
                        source = self.slot ^ b
                        gap = source - target - 1 if self.backward else target - source - 1
                        coef = jnp.where(gap >= 0, self.power(jnp.maximum(gap, 0), head), 0.0)
                        value = value + coef * self.piece(b, k, s)
                    if d == 0:
                        self.states[head, s] = value.astype(BF16)
                    else:
                        self.outs[d - 1, k, s] = value.astype(BF16)
        for d in range(1, self.width):
            self.to_owner(d).start()

    def arrive(self):
        for d in range(1, self.width):
            at = self.width + self.depth - 2 + d - 1
            self.copy(
                self.outs.at[d - 1],
                self.states.at[self.group(self.slot ^ d)],
                at,
                {"tensor": self.slot ^ d},
            ).wait_recv()

    def settle(self):
        for b in range(1, self.width):
            self.to_peer(b).wait_send()
            self.to_owner(b).wait_send()
        for j in range(1, self.depth):

            @pl.when(self.has_far(j))
            def _(j=j):
                self.to_far(j).wait_send()


def state_scratch(heads, seqs, head_dim, width, depth):
    share = heads // width
    low = functools.partial(pltpu.VMEM, dtype=BF16)
    return [
        low((heads, seqs, head_dim, head_dim)),
        low((width - 1, share, seqs, head_dim, head_dim)),
        low((share, seqs, head_dim, head_dim)),
        low((depth - 1, share, seqs, head_dim, head_dim)),
        low((width - 1, share, seqs, head_dim, head_dim)),
        pltpu.VMEM((share, seqs, head_dim, head_dim), F32),
        pltpu.SemaphoreType.DMA((2, 2 * (width - 1) + depth - 1)),
    ]


def turn(values, cosine, sine_part):
    return values * cosine + pltpu.roll(values, values.shape[-1] // 2, 1) * sine_part


def square_mean(values):
    return jnp.mean(values * values, axis=-1, keepdims=True)


def decays(rates, head, length, dim):
    rate = rates[head]
    place = lax.broadcasted_iota(jnp.int32, (length, dim), 0).astype(F32)
    query = jnp.exp(-rate[:, :dim] * (place + 1.0))
    key = jnp.exp(-rate[:, :dim] * (length - 1.0 - place))
    return query, key


def lag_decay(rates, head, length):
    lag = (
        lax.broadcasted_iota(jnp.int32, (length, length), 0)
        - lax.broadcasted_iota(jnp.int32, (length, length), 1)
    ).astype(F32)
    return jnp.where(lag >= 0, jnp.exp(-rates[head] * jnp.maximum(lag, 0.0)), 0.0)


def attend_kernel(
    depth,
    width,
    seqs,
    x,
    w_key,
    w_value,
    late_query,
    late_gate,
    late_output,
    left,
    right,
    down,
    grads,
    rates,
    powers,
    cosine,
    sine_part,
    residual,
    normed_two,
    attended,
    query_pre,
    key_pre,
    gate,
    normed_one,
    query_low,
    key_low,
    value_low,
    query_dec,
    key_dec,
    scores_low,
    gated,
    states,
    other,
    grads_nb,
    w_query,
    w_gate,
    w_output,
    local,
    came,
    total,
    far,
    outs,
    entering,
    sems,
    load_sem,
    bulk_sems,
):
    rows, model = x.shape
    length = rows // seqs
    dim = cosine.shape[1]
    tile = model // width
    loads = [
        pltpu.make_async_copy(a, b, load_sem.at[i])
        for i, (a, b) in enumerate(
            ((late_query, w_query), (late_gate, w_gate), (late_output, w_output))
        )
    ]
    for load in loads:
        load.start()
    exchange = States(
        depth, width, False, powers, local, came, total, far, outs, states, sems
    )
    core = lax.axis_index("dp")
    parity = lax.rem(exchange.place, 2)
    shard = (left, right, down)
    part_rows, part_cols = left.shape[0] // 2, model // 2
    columns_here = pl.ds(pl.multiple_of(core * part_cols, part_cols), part_cols)

    def rows_of(which):
        return pl.ds(pl.multiple_of(which * part_rows, part_rows), part_rows)

    def send(source, target, at, peer):
        return pltpu.make_async_remote_copy(
            src_ref=source,
            dst_ref=target,
            send_sem=bulk_sems.at[0, at],
            recv_sem=bulk_sems.at[1, at],
            device_id=peer,
            device_id_type=MESH,
        )

    def fetch(m):
        at = (rows_of(parity), columns_here)
        return send(
            shard[m].at[at], other.at[(m,) + at], m, {"tensor": exchange.slot ^ 2}
        )

    def relay(m):
        at = other.at[m, rows_of(parity), columns_here]
        return send(at, at, 3 + m, {"seq": exchange.place + 1 - 2 * parity})

    def share(m, which):
        spot = parity if which == 0 else 1 - parity
        at = other.at[m, rows_of(spot), columns_here]
        return send(at, at, 6 + 2 * m + which, {"dp": 1 - core})

    def cross(s):
        at = pl.ds(s * length, length)
        return send(grads.at[at], grads_nb.at[at], 12 + s, {"tensor": exchange.slot ^ 1})

    def pass_on(m):
        fetch(m).wait_recv()
        relay(m).start()
        share(m, 0).start()

    def pass_last(m):
        relay(m).wait_recv()
        share(m, 1).start()

    exchange.greet((({"dp": 1 - core}),))
    fetch(0).start()
    cross(0).start()
    fetch(1).start()
    for s in range(seqs):
        at = pl.ds(s * length, length)
        value = x[at].astype(F32)
        normed_one[at] = (value * lax.rsqrt(square_mean(value) + EPS)).astype(BF16)

    per_tile = tile // dim

    @pl.loop(1, width + 1)
    def _(step):
        b = lax.rem(step, width)
        spot = exchange.slot ^ b
        columns = pl.ds(pl.multiple_of(spot * tile, tile), tile)
        key_pre[:, columns] = times(normed_one[...], w_key[:, columns])
        value_low[:, columns] = times(normed_one[...], w_value[:, columns]).astype(BF16)
        for k in range(per_tile):
            head = spot * per_tile + k
            own = pl.ds(pl.multiple_of(spot * tile + k * dim, dim), dim)
            _, key_weight = decays(rates, head, length, dim)
            for s in range(seqs):
                at = pl.ds(s * length, length)
                turned = turn(jax.nn.silu(key_pre[at, own]), cosine[...], sine_part[...])
                key_low[at, own] = turned.astype(BF16)
                dec = (turned * key_weight).astype(BF16)
                key_dec[at, own] = dec
                local[head, s] = times_rows(dec, value_low[at, own]).astype(BF16)

        for b_static in range(1, width):

            @pl.when(b == b_static)
            def _(b_static=b_static):
                exchange.to_peer(b_static).start()

    for s in range(1, seqs):
        cross(s).start()
    fetch(2).start()
    pass_on(0)
    loads[0].wait()
    loads[1].wait()

    def inner(spot):
        columns = pl.ds(pl.multiple_of(spot * tile, tile), tile)
        query_pre[:, columns] = times(normed_one[...], w_query[:, columns])
        gate[:, columns] = times(normed_one[...], w_gate[:, columns])
        for k in range(per_tile):
            head = spot * per_tile + k
            own = pl.ds(pl.multiple_of(spot * tile + k * dim, dim), dim)
            query_weight, _ = decays(rates, head, length, dim)
            mask = lag_decay(rates, head, length)
            for s in range(seqs):
                at = pl.ds(s * length, length)
                turned = turn(jax.nn.silu(query_pre[at, own]), cosine[...], sine_part[...])
                low_query = turned.astype(BF16)
                query_low[at, own] = low_query
                query_dec[at, own] = (turned * query_weight).astype(BF16)
                low_scores = (times_back(low_query, key_low[at, own]) * mask).astype(BF16)
                scores_low[head, s] = low_scores
                attended[at, own] = times(low_scores, value_low[at, own])

    half = width // 2

    @pl.loop(0, half)
    def _(spot):
        inner(spot)

    exchange.gather()
    pass_on(1)

    @pl.loop(half, width)
    def _(spot):
        inner(spot)

    exchange.send_back(entering)
    pass_last(0)
    pass_on(2)
    loads[2].wait()
    exchange.arrive()
    pass_last(1)

    @pl.loop(0, width * per_tile)
    def _(head):
        own = pl.ds(pl.multiple_of(head * dim, dim), dim)
        for s in range(seqs):
            at = pl.ds(s * length, length)
            attended[at, own] += times(query_dec[at, own], states[head, s])

    for s in range(seqs):
        at = pl.ds(s * length, length)
        value = attended[at]
        gated[at] = (value * lax.rsqrt(square_mean(value) + EPS) * gate[at]).astype(BF16)

    @pl.loop(0, width)
    def _(spot):
        columns = pl.ds(pl.multiple_of(spot * tile, tile), tile)
        residual[:, columns] = x[:, columns].astype(F32) + times(
            gated[...], w_output[:, columns]
        )

    for s in range(seqs):
        at = pl.ds(s * length, length)
        value = residual[at]
        normed_two[at] = (value * lax.rsqrt(square_mean(value) + EPS)).astype(BF16)
    pass_last(2)
    exchange.settle()
    for m in range(3):
        fetch(m).wait_send()
        relay(m).wait_send()
        share(m, 0).wait()
        share(m, 1).wait()
    for s in range(seqs):
        cross(s).wait()


def attend(x, weights, shard, grads, rates, powers, cosine, sine_part, seqs, depth, width):
    rows, model = x.shape
    heads = rates.shape[0]
    dim = model // heads
    length = rows // seqs
    vmem = pl.BlockSpec(memory_space=pltpu.VMEM)
    anywhere = pl.BlockSpec(memory_space=pl.ANY)
    wide = jax.ShapeDtypeStruct((rows, model), F32)
    low = jax.ShapeDtypeStruct((rows, model), BF16)
    w_query, w_key, w_value, w_gate, w_output = weights
    return pl.pallas_call(
        functools.partial(attend_kernel, depth, width, seqs),
        out_shape=(wide, low, wide, wide, wide, wide)
        + (low,) * 6
        + (
            jax.ShapeDtypeStruct((heads, seqs, length, length), BF16),
            low,
            jax.ShapeDtypeStruct((heads, seqs, dim, dim), BF16),
            jax.ShapeDtypeStruct((3,) + shard[0].shape, BF16),
            low,
        ),
        in_specs=[vmem] * 3 + [anywhere] * 7 + [vmem] * 4,
        out_specs=(vmem,) * 15 + (anywhere,) * 2,
        scratch_shapes=[pltpu.VMEM((model, model), BF16)] * 3
        + state_scratch(heads, seqs, dim, width, depth)
        + [pltpu.SemaphoreType.DMA((3,)), pltpu.SemaphoreType.DMA((2, 12 + seqs))],
        compiler_params=pltpu.CompilerParams(
            collective_id=2, has_side_effects=True, vmem_limit_bytes=56 * 1024 * 1024
        ),
        name="attend",
    )(
        x,
        w_key,
        w_value,
        w_query,
        w_gate,
        w_output,
        *shard,
        grads,
        rates,
        powers,
        cosine,
        sine_part,
    )


def retreat_kernel(
    depth,
    width,
    seqs,
    residual,
    back_own,
    back_in,
    grads,
    w_output,
    attended,
    gate,
    rates,
    powers,
    cosine,
    sine_part,
    mixed_nb,
    half_nb,
    *rest,
):
    late = rest[:14]
    (
        grad_mid_low,
        gate_low,
        query_out,
        key_out,
        value_out,
        grad_tokens,
        mixed_in,
        from_y,
    ) = rest[14:22]
    held = rest[22:36]
    (
        query_low,
        key_low,
        value_low,
        query_dec,
        scores_low,
        states_in,
        query_pre,
        w_query,
        w_gate,
        key_dec,
        key_pre,
        w_key,
        w_value,
        x,
    ) = held
    (
        states,
        grad_mid,
        work,
        grad_att,
        value_part,
        key_part,
        local,
        came,
        total,
        far,
        outs,
        entering,
        sems,
        load_sem,
        bulk_sems,
    ) = rest[36:]
    rows, model = residual.shape
    length = rows // seqs
    dim = cosine.shape[1]
    tile = model // width
    per_tile = tile // dim
    loads = [
        pltpu.make_async_copy(a, b, load_sem.at[i]) for i, (a, b) in enumerate(zip(late, held))
    ]
    for load in loads:
        load.start()
    exchange = States(
        depth, width, True, powers, local, came, total, far, outs, states, sems
    )

    def send(source, target, at, peer):
        return pltpu.make_async_remote_copy(
            src_ref=source,
            dst_ref=target,
            send_sem=bulk_sems.at[0, at],
            recv_sem=bulk_sems.at[1, at],
            device_id=peer,
            device_id_type=MESH,
        )

    def cross(s):
        at = pl.ds(s * length, length)
        return send(mixed_nb.at[at], mixed_in.at[at], s, {"tensor": exchange.slot ^ 1})

    def hand(m):
        return send(half_nb.at[m], from_y.at[m], seqs + m, {"tensor": exchange.slot ^ 2})

    exchange.greet()
    cross(0).start()
    hand(0).start()

    def spans():
        return [pl.ds(s * length, length) for s in range(seqs)]

    for at in spans():
        value = residual[at]
        scale = lax.rsqrt(square_mean(value) + EPS)
        normed = value * scale
        grad = back_own[at] + back_in[at].astype(F32)
        grad = grads[at].astype(F32) + scale * (
            grad - normed * jnp.mean(grad * normed, axis=-1, keepdims=True)
        )
        grad_mid[at] = grad
        grad_mid_low[at] = grad.astype(BF16)

    def columns_of(spot):
        return pl.ds(pl.multiple_of(spot * tile, tile), tile)

    @pl.loop(0, width)
    def _(spot):
        work[:, columns_of(spot)] = times_back(grad_mid_low[...], w_output[columns_of(spot)])

    for at in spans():
        value = attended[at]
        scale = lax.rsqrt(square_mean(value) + EPS)
        normed = value * scale
        grad = work[at]
        gate_low[at] = (grad * normed).astype(BF16)
        grad = grad * gate[at]
        grad_att[at] = (
            scale * (grad - normed * jnp.mean(grad * normed, axis=-1, keepdims=True))
        ).astype(BF16)

    for load in loads[:7]:
        load.wait()

    @pl.loop(1, width + 1)
    def _(step):
        b = lax.rem(step, width)
        spot = exchange.slot ^ b
        for k in range(per_tile):
            own = pl.ds(pl.multiple_of(spot * tile + k * dim, dim), dim)
            for s, at in enumerate(spans()):
                local[spot * per_tile + k, s] = times_rows(
                    query_dec[at, own], grad_att[at, own]
                ).astype(BF16)

        for b_static in range(1, width):

            @pl.when(b == b_static)
            def _(b_static=b_static):
                exchange.to_peer(b_static).start()

    for s in range(1, seqs):
        cross(s).start()
    hand(1).start()

    def slope(values):
        sigmoid_v = jax.nn.sigmoid(values)
        return sigmoid_v * (1.0 + values * (1.0 - sigmoid_v))

    def inner(spot):
        for k in range(per_tile):
            head = spot * per_tile + k
            own = pl.ds(pl.multiple_of(spot * tile + k * dim, dim), dim)
            query_weight, _ = decays(rates, head, length, dim)
            mask = lag_decay(rates, head, length)
            for s, at in enumerate(spans()):
                grad = grad_att[at, own]
                value_part[at, own] = times_rows(scores_low[head, s], grad)
                score = (times_back(grad, value_low[at, own]) * mask).astype(BF16)
                key_part[at, own] = times_rows(score, query_low[at, own])
                turned = times(score, key_low[at, own]) + query_weight * times_back(
                    grad, states_in[head, s]
                )
                query_out[at, own] = (
                    turn(turned, cosine[...], -sine_part[...]) * slope(query_pre[at, own])
                ).astype(BF16)

    half = width // 2

    @pl.loop(0, half)
    def _(spot):
        inner(spot)

    exchange.gather()

    @pl.loop(half, width)
    def _(spot):
        inner(spot)

    exchange.send_back(entering)
    hand(2).start()
    for load in loads[7:]:
        load.wait()

    @pl.loop(0, width)
    def _(spot):
        at = columns_of(spot)
        work[:, at] = times_back(query_out[...], w_query[at]) + times_back(
            gate_low[...], w_gate[at]
        )

    exchange.arrive()

    @pl.loop(0, width * per_tile)
    def _(head):
        own = pl.ds(pl.multiple_of(head * dim, dim), dim)
        _, key_weight = decays(rates, head, length, dim)
        for s, at in enumerate(spans()):
            state = states[head, s]
            value_out[at, own] = (
                value_part[at, own] + times(key_dec[at, own], state)
            ).astype(BF16)
            turned = key_part[at, own] + key_weight * times_back(value_low[at, own], state)
            key_out[at, own] = (
                turn(turned, cosine[...], -sine_part[...]) * slope(key_pre[at, own])
            ).astype(BF16)

    @pl.loop(0, width)
    def _(spot):
        at = columns_of(spot)
        work[:, at] += times_back(key_out[...], w_key[at]) + times_back(
            value_out[...], w_value[at]
        )

    for at in spans():
        value = x[at].astype(F32)
        scale = lax.rsqrt(square_mean(value) + EPS)
        normed = value * scale
        grad = work[at]
        grad_tokens[at] = grad_mid[at] + scale * (
            grad - normed * jnp.mean(grad * normed, axis=-1, keepdims=True)
        )
    exchange.settle()
    for s in range(seqs):
        cross(s).wait()
    for m in range(3):
        hand(m).wait()


def retreat(early, tables, bulk, late, seqs, depth, width):
    rows, model = early[0].shape
    heads = tables[0].shape[0]
    dim = model // heads
    vmem = pl.BlockSpec(memory_space=pltpu.VMEM)
    anywhere = pl.BlockSpec(memory_space=pl.ANY)
    wide = jax.ShapeDtypeStruct((rows, model), F32)
    low = jax.ShapeDtypeStruct((rows, model), BF16)
    return pl.pallas_call(
        functools.partial(retreat_kernel, depth, width, seqs),
        out_shape=(low,) * 5 + (wide, low, jax.ShapeDtypeStruct(bulk[1].shape, BF16)),
        in_specs=[vmem] * (len(early) + len(tables)) + [anywhere] * (len(bulk) + len(late)),
        out_specs=(vmem,) * 6 + (anywhere,) * 2,
        scratch_shapes=[pltpu.VMEM(v.shape, v.dtype) for v in late]
        + [
            pltpu.VMEM((heads, seqs, dim, dim), BF16),
            pltpu.VMEM((rows, model), F32),
            pltpu.VMEM((rows, model), F32),
            pltpu.VMEM((rows, model), BF16),
            pltpu.VMEM((rows, model), F32),
            pltpu.VMEM((rows, model), F32),
        ]
        + state_scratch(heads, seqs, dim, width, depth)
        + [pltpu.SemaphoreType.DMA((len(late),)), pltpu.SemaphoreType.DMA((2, seqs + 3))],
        compiler_params=pltpu.CompilerParams(
            collective_id=3, has_side_effects=True, vmem_limit_bytes=60 * 1024 * 1024
        ),
        name="retreat",
    )(*early, *tables, *bulk, *late)


def on_device(
    tokens,
    w_query,
    w_key,
    w_value,
    w_ugate,
    w_output,
    w_left,
    w_right,
    w_down,
    decay_rate,
    cotangent,
):
    seq_count, group_len, model_width = tokens.shape
    head_count = decay_rate.shape[0]
    head_dim = model_width // head_count
    half_dim = head_dim // 2
    row_count = seq_count * group_len

    shard = (w_left.T, w_right.T, w_down)
    grad_own = cotangent.reshape(row_count, model_width)

    position_block = lax.axis_index(("seq", "tensor"))
    places = (position_block * group_len + jnp.arange(group_len)).astype(F32)
    frequency = 10000.0 ** (-jnp.arange(half_dim, dtype=F32) / half_dim)
    angles = places[:, None] * frequency[None, :]
    cosine, sine_part = jnp.cos(angles), jnp.sin(angles)
    cosine = jnp.concatenate([cosine, cosine], axis=1)
    sine_part = jnp.concatenate([-sine_part, sine_part], axis=1)
    rows_in = tokens.reshape(row_count, model_width)
    depth = lax.axis_size("seq")
    width = lax.axis_size("tensor")
    rates = jnp.broadcast_to(decay_rate[:, None, None], (head_count, 1, group_len))
    blocks = jnp.arange(depth * width, dtype=F32)[:, None, None, None]
    powers = jnp.broadcast_to(
        jnp.exp(-decay_rate[None, :, None, None] * group_len * blocks),
        (depth * width, head_count, 1, head_dim),
    )
    (
        residual,
        rows_own,
        merged,
        query_pre,
        key_pre,
        ugate,
        normed_low,
        query_low,
        key_low,
        value_low,
        query_dec,
        key_dec,
        weights_low,
        gated_low,
        state_low,
        other,
        grad_nb,
    ) = attend(
        rows_in,
        (w_query, w_key, w_value, w_ugate, w_output),
        shard,
        grad_own,
        rates,
        powers,
        cosine,
        sine_part,
        seq_count,
        depth,
        width,
    )
    rows_nb = swap(rows_own, "tensor", 1)

    mixed_own, back_own, kept = hidden_part(rows_own, grad_own, shard + (other,), None, F32)
    mixed_nb, back_nb, kept = hidden_part(rows_nb, grad_nb, shard + (other,), kept, BF16)
    back_in = swap(back_nb, "tensor", 1)
    mine, theirs = hidden_grads(kept[1], rows_own, rows_nb, grad_own, grad_nb)
    moved = swap(theirs, "dp", 1)
    half_nb = added(mine, moved)
    mine, theirs = hidden_grads(kept[0], rows_own, rows_nb, grad_own, grad_nb)
    moved = swap(theirs, "dp", 1)

    (
        grad_branch,
        grad_ugate_pre,
        grad_query_pre,
        grad_key_pre,
        grad_value_pre,
        grad_tokens,
        mixed_in,
        from_y,
    ) = retreat(
        (residual, back_own, back_in, grad_own, w_output, merged, ugate),
        (rates, powers, cosine, sine_part),
        (mixed_nb, half_nb),
        (
            query_low,
            key_low,
            value_low,
            query_dec,
            weights_low,
            state_low,
            query_pre,
            w_query,
            w_ugate,
            key_dec,
            key_pre,
            w_key,
            w_value,
            rows_in,
        ),
        seq_count,
        depth,
        width,
    )

    def weight_grad(rows, gradient):
        return jnp.einsum("rd,re->de", rows, gradient, preferred_element_type=F32)

    partial = (
        weight_grad(normed_low, grad_query_pre),
        weight_grad(normed_low, grad_key_pre),
        weight_grad(normed_low, grad_value_pre),
        weight_grad(normed_low, grad_ugate_pre),
        weight_grad(gated_low, grad_branch),
    )
    shard_half = (mine.astype(F32) + moved.astype(F32) + from_y.astype(F32)).astype(BF16)
    hidden = w_down.shape[0]
    sums, hidden_sums = reduce_grads(
        tuple(g.astype(BF16) for g in partial),
        shard_half.reshape(3 * hidden, model_width // 2),
        lax.axis_size("seq"),
    )
    mixed_out = (residual + mixed_own + mixed_in.astype(F32)).astype(BF16)
    attention_grads = tuple(
        sums[i * model_width : (i + 1) * model_width].astype(F32) for i in range(len(partial))
    )
    left_sum, right_sum, down_sum = (
        hidden_sums[i * hidden : (i + 1) * hidden].astype(F32) for i in range(3)
    )
    return (
        (mixed_out.reshape(tokens.shape), grad_tokens.reshape(tokens.shape))
        + attention_grads
        + (left_sum.T, right_sum.T, down_sum)
    )


def solution(mesh):
    rows = P("dp", ("seq", "tensor"), None)
    columns = P(None, "tensor")
    return jax.shard_map(
        on_device,
        mesh=mesh,
        in_specs=(rows, P(), P(), P(), P(), P(), columns, columns, P("tensor", None), P(), rows),
        out_specs=(rows, rows, P(), P(), P(), P(), P(), columns, columns, P("tensor", None)),
        check_vma=False,
    )
```

profile of v0, /device:TPU:0, one launch (start us, length us, event | category | flops | bytes accessed | tf_op | source)
XLA Modules:
  0.0 375.2 jit_solution(16964029806681018290)
XLA Ops:
  0.7 0.7 negate_multiply_fusion
  1.3 0.5 fusion
  1.9 0.8 pad_maximum_fusion
  2.7 1.3 broadcast_in_dim.4.rates
  4.1 0.8 broadcast_in_dim.5.powers
  4.9 62.3 %attend.1 = (f32[512,1024]{1,0:T(8,128)}, bf16[512,1024]{1,0:T(8,128)(2,1)}, f32[512,1024]{1,0:T(8,128)}, f32[512,1024]{1,0:T(8,128)}, f32[512,1024]{1,0:T(8,128...) custom-call(bf16[512,1024]{1,0:T(8,128)(2,1)} %bitcast.27, ...), custom_call_target="tpu_custom_call" | custom-call | tf_op jit(solution)/shard_map/attend/pallas_call | solution.py:930
  67.2 1.6 collective-permute-start
  68.7 15.9 %hidden_part.2 = (f32[512,1024]{1,0:T(8,128)}, f32[512,1024]{1,0:T(8,128)}, bf16[3,1024,704]{2,1,0:T(8,128)(2,1)}, bf16[3,1024,704]{2,1,0:T(8,128)(2,1)}) custom-call(bf16[512,1024]{1,0:T(8,128)(2,1)} %get-tuple-element.50.refs_0_.rows_own, bf16[512,1024]{1,0:T(8,128)(2,1)} %bitcast.22, bf16[704,1024]{1,0:T(8,128)(2,1)} %bitcast.31, ...), custom_call_target="tpu_custom_call" | custom-call | flops 8858370048 | bytes 19267584 | tf_op jit(solution)/shard_map/hidden_part/pallas_call | solution.py:440
  84.7 5.3 %collective-permute-done.refs_0_.rows_nb = bf16[512,1024]{1,0:T(8,128)(2,1)S(1)} collective-permute-done((bf16[512,1024]{1,0:T(8,128)(2,1)}, bf16[512,1024]{1,0:T(8,128)(2,1)S(1)}, u32[]{:S(2)}, u32[]{:S(2)}) %collective-permute-start) | collective-permute-done | bytes 1048608 | tf_op jit(solution)/shard_map/ppermute | solution.py:19
  89.9 0.0 copy-start.3
  89.9 1.0 copy-done.3
  90.9 0.0 copy-start
  90.9 0.0 copy-start.2
  90.9 15.9 %hidden_part.3 = (bf16[512,1024]{1,0:T(8,128)(2,1)}, bf16[512,1024]{1,0:T(8,128)(2,1)}, bf16[3,1024,704]{2,1,0:T(8,128)(2,1)}, bf16[3,1024,704]{2,1,0:T(8,128)(2,1)}) custom-call(bf16[512,1024]{1,0:T(8,128)(2,1)} %copy-done.3, bf16[512,1024]{1,0:T(8,128)(2,1)} %get-tuple-element.54.refs_1_.grads_nb, ...), custom_call_target="tpu_custom_call", output_to_operand_aliasing={{2}: (6, {}), {3}: (7, {})} | custom-call | flops 8858370048 | bytes 19267584 | tf_op jit(solution)/shard_map/hidden_part/pallas_call | solution.py:440
  106.8 0.0 copy-done
  106.8 0.0 copy-done.1
  106.8 0.0 copy-done.2
  106.8 0.0 copy-start.4
  106.8 1.2 copy-done.4
  108.0 0.0 copy-start.6
  108.0 2.3 copy-done.6
  110.3 0.0 copy-start.15
  110.3 5.9 %hidden_grads.2 = (bf16[3,704,512]{2,1,0:T(8,128)(2,1)S(1)}, bf16[3,704,512]{2,1,0:T(8,128)(2,1)S(1)}) custom-call(bf16[3,1024,704]{2,1,0:T(8,128)(2,1)S(1)} %copy-done.6, bf16[512,1024]{1,0:T(8,128)(2,1)S(1)} %copy-done.1, bf16[512,1024]{1,0:T(8,128)(2,1)S(1)} %copy-done.4, bf16[512,1024]{1,0:T(8,128)(2,1)S(1)} %bitcast.24, bf16[512,1024]{1,0:T(8,128)(2,1)S(1)} %copy-done.2), custom_call_target="tpu_custom_call" | custom-call | flops 4429185024 | bytes 12845056 | tf_op jit(solution)/shard_map/hidden_grads/pallas_call | solution.py:489
  116.3 0.1 collective-permute-start.2
  116.3 0.0 copy-done.15
  116.3 1.6 collective-permute-start.1
  117.9 0.0 copy-start.5
  117.9 2.3 copy-done.5
  120.2 6.6 %hidden_grads.3 = (bf16[3,704,512]{2,1,0:T(8,128)(2,1)S(1)}, bf16[3,704,512]{2,1,0:T(8,128)(2,1)}) custom-call(bf16[3,1024,704]{2,1,0:T(8,128)(2,1)S(1)} %copy-done.5, bf16[512,1024]{1,0:T(8,128)(2,1)S(1)} %copy-done.1, bf16[512,1024]{1,0:T(8,128)(2,1)S(1)} %copy-done.4, bf16[512,1024]{1,0:T(8,128)(2,1)S(1)} %bitcast.25, bf16[512,1024]{1,0:T(8,128)(2,1)S(1)} %copy-done.2), custom_call_target="tpu_custom_call" | custom-call | flops 4429185024 | bytes 12845056 | tf_op jit(solution)/shard_map/hidden_grads/pallas_call | solution.py:489
  126.9 0.2 collective-permute-start.3
  127.0 0.0 collective-permute-done.2
  127.0 2.0 add_convert_fusion.1.half_nb
  129.0 13.0 %collective-permute-done.1.back_in = bf16[512,1024]{1,0:T(8,128)(2,1)} collective-permute-done((bf16[512,1024]{1,0:T(8,128)(2,1)S(1)}, bf16[512,1024]{1,0:T(8,128)(2,1)}, u32[]{:S(2)}, u32[]{:S(2)}) %collective-permute-start.1) | collective-permute-done | bytes 1048608 | tf_op jit(solution)/shard_map/ppermute | solution.py:19
  142.0 0.0 copy-start.14
  142.0 74.6 %retreat.1 = (bf16[512,1024]{1,0:T(8,128)(2,1)}, bf16[512,1024]{1,0:T(8,128)(2,1)}, bf16[512,1024]{1,0:T(8,128)(2,1)}, bf16[512,1024]{1,0:T(8,128)(2,1)}, bf16[5...) custom-call(f32[512,1024]{1,0:T(8,128)} %get-tuple-element.49.residual, ...), custom_call_target="tpu_custom_call" | custom-call | tf_op jit(solution)/shard_map/retreat/pallas_call | solution.py:1213
  216.6 0.0 copy-done.14
  216.6 0.0 copy-start.19
  216.7 3.9 %convolution_convert_fusion.4.refs_0_ = bf16[1024,1024]{1,0:T(8,128)(2,1)} fusion(bf16[512,1024]{1,0:T(8,128)(2,1)S(1)} %copy-done.14, bf16[512,1024]{1,0:T(8,128)(2,1)} %get-tuple-element.76), kind=kOutput, calls=%fused_computation.14 | convolution fusion | flops 1074790400 | bytes 4194304 | tf_op jit(solution)/shard_map/rd,re->de/dot_general | solution.py:1351
  220.6 0.0 copy-done.19
  220.6 0.0 copy-start.18
  220.6 2.6 convolution_convert_fusion.3.refs_1_
  223.2 0.0 copy-done.18
  223.2 0.0 copy-start.17
  223.2 2.6 convolution_convert_fusion.2.refs_2_
  225.8 0.0 copy-done.17
  225.9 2.6 convolution_convert_fusion.1.refs_3_
  228.5 0.0 copy-done.13
  228.5 0.0 copy-done.16
  228.5 2.6 convolution_convert_fusion.refs_4_
  231.1 0.0 collective-permute-done.3
  231.1 0.0 copy-done.9
  231.1 3.9 %add_convert_fusion = bf16[3,704,512]{2,1,0:T(8,128)(2,1)} fusion(bf16[3,704,512]{2,1,0:T(8,128)(2,1)S(1)} %copy-done.9, bf16[3,704,512]{2,1,0:T(8,128)(2,1)} %collective-permute-done.3, bf16[3,704,512]{2,1,0:T(8,128)(2,1)S(1)} %get-tuple-element.83), kind=kLoop, calls=%fused_computation | loop fusion | flops 6488064 | bytes 8650752 | tf_op jit(solution)/shard_map/convert_element_type | solution.py:1360
  235.0 120.4 %reduce_grads.1 = (bf16[5120,1024]{1,0:T(8,128)(2,1)}, bf16[2112,1024]{1,0:T(8,128)(2,1)}) custom-call(bf16[1024,1024]{1,0:T(8,128)(2,1)} %convolution_convert_fusion.4.refs_0_, bf16[1024,1024]{1,0:T(8,128)(2,1)} %convolution_convert_fusion.3.refs_1_, bf16[1024,1024]{1,0:T(8,128)(2,1)} %convolution_convert_fusion.2.refs_2_, ...), custom_call_target="tpu_custom_call" | custom-call | tf_op jit(solution)/shard_map/reduce_grads/pallas_call | solution.py:364
  355.3 0.0 copy-start.7
  355.4 7.1 %slice_convert_fusion.5 = (f32[704,1024]{1,0:T(8,128)}, f32[1024,704]{0,1:T(8,128)}, f32[1024,704]{0,1:T(8,128)}) fusion(bf16[2112,1024]{1,0:T(8,128)(2,1)} %get-tuple-element.87), kind=kLoop, calls=%fused_computation.15 | loop fusion | flops 2162688 | bytes 12976128 | tf_op jit(solution)/shard_map/convert_element_type | solution.py:1372
  362.4 1.3 copy-done.7
  363.7 8.3 %slice_convert_fusion = (f32[1024,1024]{1,0:T(8,128)}, f32[1024,1024]{1,0:T(8,128)}, f32[1024,1024]{1,0:T(8,128)}, f32[1024,1024]{1,0:T(8,128)}, f32[1024,1024]{1,0:T(8,128)}) fusion(bf16[5120,1024]{1,0:T(8,128)(2,1)S(1)} %copy-done.7), kind=kLoop, calls=%fused_computation.4 | loop fusion | flops 5242880 | bytes 31457280 | tf_op jit(solution)/shard_map/convert_element_type | solution.py:1369
  371.9 0.0 copy-done.8
  372.0 0.0 copy-done.10
  372.0 0.0 copy-done.12
  372.0 0.0 copy-start.11
  372.0 1.6 add_convert_fusion.2
  373.6 0.0 copy-done.11
  373.6 1.3 copy.26
  (10 shorter events, 0.0 us)
Async XLA Ops:
  67.2 22.8 %collective-permute-start = (bf16[512,1024]{1,0:T(8,128)(2,1)}, bf16[512,1024]{1,0:T(8,128)(2,1)S(1)}, u32[]{:S(2)}, u32[]{:S(2)}) collective-permute-start(bf16[512,1024]{1,0:T(8,128)(2,1)} %get-tuple-element.50.refs_0_.rows_own), channel_id=1, source_target_pairs={{0,1},{1,0},{2,3},{3,2},{4,5},{5,4},{6,7},{7,6},{8,9},{9,8},{10,11... | collective-permute-start | bytes 3145736 | tf_op jit(solution)/shard_map/ppermute | solution.py:19
  89.9 1.0 copy-start.3
  90.9 15.9 %copy-start = (bf16[2,256,1024]{2,1,0:T(8,128)(2,1)S(1)}, bf16[2,256,1024]{2,1,0:T(8,128)(2,1)}, u32[]{:S(2)}) copy-start(bf16[2,256,1024]{2,1,0:T(8,128)(2,1)} %param.21) | copy-start | bytes 3145732
  90.9 15.9 %copy-start.1 = (bf16[512,1024]{1,0:T(8,128)(2,1)S(1)}, bf16[512,1024]{1,0:T(8,128)(2,1)}, u32[]{:S(2)}) copy-start(bf16[512,1024]{1,0:T(8,128)(2,1)} %get-tuple-element.50.refs_0_.rows_own) | copy-start | bytes 3145732
  90.9 15.9 %copy-start.2 = (bf16[512,1024]{1,0:T(8,128)(2,1)S(1)}, bf16[512,1024]{1,0:T(8,128)(2,1)}, u32[]{:S(2)}) copy-start(bf16[512,1024]{1,0:T(8,128)(2,1)} %get-tuple-element.54.refs_1_.grads_nb) | copy-start | bytes 3145732
  106.8 1.2 copy-start.4
  108.0 2.3 copy-start.6
  110.3 6.0 %copy-start.15 = (bf16[512,1024]{1,0:T(8,128)(2,1)S(1)}, bf16[512,1024]{1,0:T(8,128)(2,1)}, u32[]{:S(2)}) copy-start(bf16[512,1024]{1,0:T(8,128)(2,1)} %get-tuple-element.57) | copy-start | bytes 3145732
  116.3 10.8 %collective-permute-start.2 = (bf16[3,704,512]{2,1,0:T(8,128)(2,1)S(1)}, bf16[3,704,512]{2,1,0:T(8,128)(2,1)S(1)}, u32[]{:S(2)}, u32[]{:S(2)}) collective-permute-start(bf16[3,704,512]{2,1,0:T(8,128)(2,1)S(1)} %get-tuple-element.63), channel_id=1, source_target_pairs={{0,16},{16,0},{1,17},{17,1},{2,18},{18,2},{3,19},{19,3},{4,20},{20... | collective-permute-start | bytes 6488072 | tf_op jit(solution)/shard_map/ppermute | solution.py:19
  116.3 25.7 %collective-permute-start.1 = (bf16[512,1024]{1,0:T(8,128)(2,1)S(1)}, bf16[512,1024]{1,0:T(8,128)(2,1)}, u32[]{:S(2)}, u32[]{:S(2)}) collective-permute-start(bf16[512,1024]{1,0:T(8,128)(2,1)S(1)} %copy-done.15), channel_id=1, source_target_pairs={{0,1},{1,0},{2,3},{3,2},{4,5},{5,4},{6,7},{7,6},{8,9},{9,8},{10,11... | collective-permute-start | bytes 3145736 | tf_op jit(solution)/shard_map/ppermute | solution.py:19
  117.9 2.3 copy-start.5
  126.9 104.2 %collective-permute-start.3 = (bf16[3,704,512]{2,1,0:T(8,128)(2,1)}, bf16[3,704,512]{2,1,0:T(8,128)(2,1)}, u32[]{:S(2)}, u32[]{:S(2)}) collective-permute-start(bf16[3,704,512]{2,1,0:T(8,128)(2,1)} %get-tuple-element.84), channel_id=1, source_target_pairs={{0,16},{16,0},{1,17},{17,1},{2,18},{18,2},{3,19},{19,3},{4,20},{20... | collective-permute-start | bytes 6488072 | tf_op jit(solution)/shard_map/ppermute | solution.py:19
  142.0 74.6 %copy-start.14 = (bf16[512,1024]{1,0:T(8,128)(2,1)S(1)}, bf16[512,1024]{1,0:T(8,128)(2,1)}, u32[]{:S(2)}) copy-start(bf16[512,1024]{1,0:T(8,128)(2,1)} %get-tuple-element.75) | copy-start | bytes 3145732
  216.6 3.9 %copy-start.19 = (bf16[512,1024]{1,0:T(8,128)(2,1)S(1)}, bf16[512,1024]{1,0:T(8,128)(2,1)}, u32[]{:S(2)}) copy-start(bf16[512,1024]{1,0:T(8,128)(2,1)} %get-tuple-element.77) | copy-start | bytes 3145732
  220.6 2.6 copy-start.18
  223.2 2.6 copy-start.17
  225.8 2.6 copy-start.13
  225.8 2.6 copy-start.16
  228.5 2.6 copy-start.9
  355.3 8.3 %copy-start.7 = (bf16[5120,1024]{1,0:T(8,128)(2,1)S(1)}, bf16[5120,1024]{1,0:T(8,128)(2,1)}, u32[]{:S(2)}) copy-start(bf16[5120,1024]{1,0:T(8,128)(2,1)} %get-tuple-element.86) | copy-start | bytes 31457284
  363.7 8.3 %copy-start.8 = (f32[512,1024]{1,0:T(8,128)S(1)}, f32[512,1024]{1,0:T(8,128)}, u32[]{:S(2)}) copy-start(f32[512,1024]{1,0:T(8,128)} %get-tuple-element.49.residual) | copy-start | bytes 6291460
  363.7 8.3 %copy-start.10 = (f32[512,1024]{1,0:T(8,128)S(1)}, f32[512,1024]{1,0:T(8,128)}, u32[]{:S(2)}) copy-start(f32[512,1024]{1,0:T(8,128)} %get-tuple-element.52) | copy-start | bytes 6291460
  363.7 8.3 %copy-start.12 = (bf16[512,1024]{1,0:T(8,128)(2,1)S(1)}, bf16[512,1024]{1,0:T(8,128)(2,1)}, u32[]{:S(2)}) copy-start(bf16[512,1024]{1,0:T(8,128)(2,1)} %get-tuple-element.73) | copy-start | bytes 3145732
  372.0 1.6 copy-start.11
where the time goes:
time: 379 us; the launch traced here: 375 us
  Pallas kernels  302 us (80%)
  other arithmetic  24.8 us (7%)
  waiting for transfers between devices  18.3 us (5%)
  matrix products  14.4 us (4%)
  local copies, waits for them, and re-layouts  11.7 us (3%)
    pallas_call x1, Pallas kernels, reduce_grads(): pl.pallas_call(body, out_shape=(jax.ShapeDtypeStruct((rows, width), BF16)...  120 us
    pallas_call x1, Pallas kernels, retreat(): pl.pallas_call(functools.partial(retreat_kernel, depth, width, seqs), out...  74.6 us
    pallas_call x1, Pallas kernels, attend(): pl.pallas_call(functools.partial(attend_kernel, depth, width, seqs), out_...  62.3 us
    pallas_call x2, Pallas kernels, hidden_part(): pl.pallas_call(body, grid=(count // ROWS,), out_shape=(jax.ShapeDtypeStru...  31.8 us
    ppermute x4, waiting for transfers between devices, swap(): lax.ppermute(v, axis, [(i, i ^ bit) for i in range(count)])  18.3 us
    dot_general x5, matrix products, weight_grad(): return jnp.einsum('rd,re->de', rows, gradient, preferred_element_type=F32)  14.4 us
    pallas_call x2, Pallas kernels, hidden_grads(): pl.pallas_call(hidden_grads_kernel, grid=(3,), out_shape=(jax.ShapeDtypeS...  12.5 us
    unnamed x41, local copies, waits for them, and re-layouts  9.5 us
  transfers between devices with their start and end apart: 4, of which 2 were waited for; matrix products, arithmetic and copies ran while one was open for 4% of the time, Pallas kernels for 26%

commit v1 on v0

--- a/solution.py
+++ b/solution.py
@@ -13,15 +13,8 @@
 BF16 = jnp.bfloat16
 
 
-def swap(value, axis, bit):
-    count = lax.axis_size(axis)
-    return jax.tree.map(
-        lambda v: lax.ppermute(v, axis, [(i, i ^ bit) for i in range(count)]), value
-    )
-
-
 CHUNK = 256
-LAG = 2
+LAG = 1
 
 
 def added(first, second):
@@ -31,9 +24,12 @@
 def reduce_kernel(
     depth,
     grads,
-    pair_in,
+    pair_own,
+    pair_first,
+    pair_rest,
     out,
     pair_out,
+    pair_in,
     own,
     core_in,
     first_in,
@@ -266,6 +262,11 @@
         def _(q):
             to_core(q).start()
 
+    hidden = pair_first.shape[0]
+    for m in range(3):
+        theirs = pair_first[...] if m == 0 else pair_rest[m - 1]
+        pair_in[pl.ds(m * hidden, hidden)] = added(pair_own[m], theirs)
+
     def stage_a(q):
         to_core(q).wait_recv()
         came = core_in.at[q]
@@ -350,12 +351,13 @@
         pair.settle(q)
 
 
-def reduce_grads(grads, pair_half, depth):
+def reduce_grads(grads, half_own, first_y, rest_y, depth):
     size, width = grads[0].shape
     rows = size * len(grads)
     chunks = rows // CHUNK
     pair_chunks = 12
-    pair_rows, pair_cols = pair_half.shape[0] // pair_chunks, pair_half.shape[1]
+    total_rows, pair_cols = 3 * half_own.shape[1], half_own.shape[2]
+    pair_rows = total_rows // pair_chunks
     vmem = pl.BlockSpec(memory_space=pltpu.VMEM)
 
     def body(*refs):
@@ -365,11 +367,12 @@
         body,
         out_shape=(
             jax.ShapeDtypeStruct((rows, width), BF16),
-            jax.ShapeDtypeStruct((pair_half.shape[0], 2 * pair_cols), BF16),
+            jax.ShapeDtypeStruct((total_rows, 2 * pair_cols), BF16),
         ),
-        in_specs=[pl.BlockSpec(memory_space=pl.ANY)] * len(grads) + [vmem],
+        in_specs=[pl.BlockSpec(memory_space=pl.ANY)] * len(grads) + [vmem] * 3,
         out_specs=(vmem, vmem),
         scratch_shapes=[
+            pltpu.VMEM((total_rows, pair_cols), BF16),
             pltpu.VMEM((rows, width), BF16),
             pltpu.VMEM((chunks, CHUNK // 2, width), BF16),
             pltpu.VMEM((chunks, CHUNK // 4, width), BF16),
@@ -383,10 +386,10 @@
             pltpu.SemaphoreType.DMA((len(grads),)),
         ],
         compiler_params=pltpu.CompilerParams(
-            collective_id=1, has_side_effects=True, vmem_limit_bytes=60 * 1024 * 1024
+            collective_id=1, has_side_effects=True, vmem_limit_bytes=50 * 1024 * 1024
         ),
         name="reduce_grads",
-    )(*grads, pair_half)
+    )(*grads, half_own, first_y, rest_y)
 
 
 ROWS = 256
@@ -404,102 +407,174 @@
     return lax.dot_general(x, y, (((0,), (0,)), ((), ())), preferred_element_type=F32)
 
 
-def hidden_kernel(rows, grads, left, right, down, other, *rest):
-    mixed, back, own_kept, other_kept, acc_mixed, acc_back = rest[-6:]
-
-    def unit(kept, w_left, w_right, w_down):
-        e1, e2 = times_back(rows[...], w_left), times_back(rows[...], w_right)
-        dm = times_back(grads[...], w_down)
-        kept[2] = (e1 * e2).astype(BF16)
-        kept[0] = (dm * e2).astype(BF16)
-        kept[1] = (dm * e1).astype(BF16)
-        return times(kept[2], w_down), times(kept[0], w_left) + times(kept[1], w_right)
-
-    acc_mixed[...], acc_back[...] = unit(own_kept, left[...], right[...], down[...])
-    more_mixed, more_back = unit(other_kept, other[0], other[1], other[2])
-    mixed[...] = (acc_mixed[...] + more_mixed).astype(mixed.dtype)
-    back[...] = (acc_back[...] + more_back).astype(back.dtype)
-
-
-def hidden_part(rows, grads, weights, kept, out_type):
-    count, width = rows.shape
-    hidden = weights[0].shape[0]
-    first = 0 if kept is None else count // ROWS
-
-    def whole(array):
-        return pl.BlockSpec(array.shape, lambda i: (0,) * array.ndim)
-
-    row_spec = pl.BlockSpec((ROWS, width), lambda i: (i, 0))
-    kept_spec = pl.BlockSpec((3, ROWS, hidden), lambda i: (0, i + first, 0))
-    extra = [] if kept is None else list(kept)
-    held = 2 + len(weights)
-
-    def body(*refs):
-        hidden_kernel(*refs[:held], *refs[held + len(extra) :])
-
-    outs = pl.pallas_call(
-        body,
-        grid=(count // ROWS,),
-        out_shape=(jax.ShapeDtypeStruct((count, width), out_type),) * 2
-        + (jax.ShapeDtypeStruct((3, 2 * count, hidden), BF16),) * 2,
-        in_specs=[row_spec, row_spec]
-        + [whole(w) for w in weights]
-        + [pl.BlockSpec(memory_space=pl.ANY)] * len(extra),
-        out_specs=(row_spec, row_spec, kept_spec, kept_spec),
-        scratch_shapes=[pltpu.VMEM((ROWS, width), F32), pltpu.VMEM((ROWS, width), F32)],
-        input_output_aliases={held + i: 2 + i for i in range(len(extra))},
-        compiler_params=pltpu.CompilerParams(vmem_limit_bytes=56 * 1024 * 1024),
-        cost_estimate=pl.CostEstimate(
-            flops=24 * count * width * hidden,
-            bytes_accessed=12 * width * hidden + 12 * count * hidden + 12 * count * width,
-            transcendentals=0,
+def hidden_kernel(
+    rows_own,
+    grads_own,
+    grads_nb,
+    late_left,
+    late_right,
+    late_down,
+    late_other,
+    mixed,
+    back,
+    half_own,
+    half_nb,
+    back_in,
+    from_y,
+    both,
+    own,
+    other,
+    kept,
+    theirs,
+    moved,
+    acc_mixed,
+    acc_back,
+    load_sem,
+    sems,
+):
+    core = lax.axis_index("dp")
+    slot = lax.axis_index("tensor")
+    count, width = rows_own.shape
+    half = width // 2
+    blocks = count // ROWS
+    pairs = (
+        (late_left, own.at[0]),
+        (late_right, own.at[1]),
+        (late_down, own.at[2]),
+        (late_other, other),
+        (rows_own, both.at[0, :count]),
+        (grads_own, both.at[1, :count]),
+        (grads_nb, both.at[1, count:]),
+    )
+    loads = [pltpu.make_async_copy(a, b, load_sem.at[i]) for i, (a, b) in enumerate(pairs)]
+    for i in (4, 5, 0, 1, 2, 3, 6):
+        loads[i].start()
+
+    def send(source, target, at, peer):
+        return pltpu.make_async_remote_copy(
+            src_ref=source,
+            dst_ref=target,
+            send_sem=sems.at[0, at],
+            recv_sem=sems.at[1, at],
+            device_id=peer,
+            device_id_type=MESH,
+        )
+
+    def span(i):
+        return pl.ds(pl.multiple_of(i * ROWS, ROWS), ROWS)
+
+    def out_rows(i):
+        return send(
+            rows_own.at[span(i)], both.at[0, span(blocks + i)], i, {"tensor": slot ^ 1}
+        )
+
+    def return_rows(i):
+        return send(
+            back.at[span(blocks + i)], back_in.at[span(i)], blocks + i, {"tensor": slot ^ 1}
+        )
+
+    def to_core(which, m):
+        return send(
+            theirs.at[which, m], moved.at[which, m], 2 * blocks + 3 * which + m, {"dp": 1 - core}
+        )
+
+    hand = send(half_nb.at[0], from_y, 2 * blocks + 6, {"tensor": slot ^ 2})
+    barrier = pltpu.get_barrier_semaphore()
+    for peer in ({"tensor": slot ^ 1}, {"tensor": slot ^ 2}, {"dp": 1 - core}):
+        pl.semaphore_signal(barrier, inc=1, device_id=peer, device_id_type=MESH)
+    pl.semaphore_wait(barrier, 3)
+    for i in range(blocks):
+        out_rows(i).start()
+    for load in loads:
+        load.wait()
+
+    def unit(i, which, weights):
+        rows, grads = both[0, span(i)], both[1, span(i)]
+        e1, e2 = times_back(rows, weights[0]), times_back(rows, weights[1])
+        dm = times_back(grads, weights[2])
+        mid = (e1 * e2).astype(BF16)
+        de1 = (dm * e2).astype(BF16)
+        de2 = (dm * e1).astype(BF16)
+        kept[which, 2, span(i)] = mid
+        kept[which, 0, span(i)] = de1
+        kept[which, 1, span(i)] = de2
+        return times(mid, weights[2]), times(de1, weights[0]) + times(de2, weights[1])
+
+    @pl.loop(0, 2 * blocks)
+    def _(i):
+        @pl.when(i >= blocks)
+        def _():
+            out_rows(i - blocks).wait_recv()
+
+        acc_mixed[...], acc_back[...] = unit(i, 0, own)
+        more_mixed, more_back = unit(i, 1, other)
+        mixed[span(i)] = (acc_mixed[...] + more_mixed).astype(BF16)
+        back[span(i)] = (acc_back[...] + more_back).astype(BF16)
+
+        @pl.when(i >= blocks)
+        def _():
+            return_rows(i - blocks).start()
+
+    here = pl.ds(pl.multiple_of(core * half, half), half)
+    there = pl.ds(pl.multiple_of((1 - core) * half, half), half)
+    for which, out in ((1, half_nb), (0, half_own)):
+
+        @pl.loop(0, 3)
+        def _(m, which=which, out=out):
+            theirs[which, m] = times_rows(kept[which, m], both[m // 2, :, there]).astype(BF16)
+            to_core(which, m).start()
+            out[m] = times_rows(kept[which, m], both[m // 2, :, here]).astype(BF16)
+
+        for m in range(3):
+            to_core(which, m).wait_recv()
+            out[m] = added(out[m], moved[which, m])
+        if which == 1:
+            hand.start()
+    for i in range(blocks):
+        out_rows(i).wait_send()
+        return_rows(i).wait()
+    for which in range(2):
+        for m in range(3):
+            to_core(which, m).wait_send()
+    hand.wait()
+
+
+def hidden_part(rows_own, grads_own, grads_nb, shard, other):
+    count, width = rows_own.shape
+    hidden = shard[0].shape[0]
+    vmem = pl.BlockSpec(memory_space=pltpu.VMEM)
+    anywhere = pl.BlockSpec(memory_space=pl.ANY)
+    half = jax.ShapeDtypeStruct((3, hidden, width // 2), BF16)
+    two = jax.ShapeDtypeStruct((2 * count, width), BF16)
+    return pl.pallas_call(
+        hidden_kernel,
+        out_shape=(
+            two,
+            two,
+            half,
+            half,
+            jax.ShapeDtypeStruct((count, width), BF16),
+            jax.ShapeDtypeStruct((hidden, width // 2), BF16),
+        ),
+        in_specs=[anywhere] * 7,
+        out_specs=(vmem,) * 4 + (anywhere,) * 2,
+        scratch_shapes=[
+            pltpu.VMEM((2, 2 * count, width), BF16),
+            pltpu.VMEM((3, hidden, width), BF16),
+            pltpu.VMEM((3, hidden, width), BF16),
+            pltpu.VMEM((2, 3, 2 * count, hidden), BF16),
+            pltpu.VMEM((2, 3, hidden, width // 2), BF16),
+            pltpu.VMEM((2, 3, hidden, width // 2), BF16),
+            pltpu.VMEM((ROWS, width), F32),
+            pltpu.VMEM((ROWS, width), F32),
+            pltpu.SemaphoreType.DMA((7,)),
+            pltpu.SemaphoreType.DMA((2, 2 * (count // ROWS) + 7)),
+        ],
+        compiler_params=pltpu.CompilerParams(
+            collective_id=4, has_side_effects=True, vmem_limit_bytes=54 * 1024 * 1024
         ),
         name="hidden_part",
-    )(rows, grads, *weights, *extra)
-    return outs[0], outs[1], outs[2:]
-
-
-def hidden_grads_kernel(kept, rows_own, rows_nb, grads_own, grads_nb, mine, theirs):
-    core = lax.axis_index("dp")
-    half = mine.shape[2]
-    count = rows_own.shape[0]
-    for out, which in ((mine, core), (theirs, 1 - core)):
-        at = pl.ds(pl.multiple_of(which * half, half), half)
-
-        @pl.when(pl.program_id(0) < 2)
-        def _(out=out, at=at):
-            out[0] = (
-                times_rows(kept[0, :count], rows_own[:, at])
-                + times_rows(kept[0, count:], rows_nb[:, at])
-            ).astype(BF16)
-
-        @pl.when(pl.program_id(0) == 2)
-        def _(out=out, at=at):
-            out[0] = (
-                times_rows(kept[0, :count], grads_own[:, at])
-                + times_rows(kept[0, count:], grads_nb[:, at])
-            ).astype(BF16)
-
-
-def hidden_grads(kept, rows_own, rows_nb, grads_own, grads_nb):
-    count, width = rows_own.shape
-    hidden = kept.shape[2]
-    whole = pl.BlockSpec((count, width), lambda i: (0, 0))
-    out_spec = pl.BlockSpec((1, hidden, width // 2), lambda i: (i, 0, 0))
-    return pl.pallas_call(
-        hidden_grads_kernel,
-        grid=(3,),
-        out_shape=(jax.ShapeDtypeStruct((3, hidden, width // 2), BF16),) * 2,
-        in_specs=[pl.BlockSpec((1, 2 * count, hidden), lambda i: (i, 0, 0))] + [whole] * 4,
-        out_specs=(out_spec, out_spec),
-        compiler_params=pltpu.CompilerParams(vmem_limit_bytes=40 * 1024 * 1024),
-        cost_estimate=pl.CostEstimate(
-            flops=12 * count * width * hidden,
-            bytes_accessed=12 * count * hidden + 8 * count * width + 6 * width * hidden,
-            transcendentals=0,
-        ),
-        name="hidden_grads",
-    )(kept, rows_own, rows_nb, grads_own, grads_nb)
+    )(rows_own, grads_own, grads_nb, *shard, other)
 
 
 MESH = pl.DeviceIdType.MESH
@@ -1053,10 +1128,13 @@
 
     def cross(s):
         at = pl.ds(s * length, length)
-        return send(mixed_nb.at[at], mixed_in.at[at], s, {"tensor": exchange.slot ^ 1})
+        source = mixed_nb.at[pl.ds(rows + s * length, length)]
+        return send(source, mixed_in.at[at], s, {"tensor": exchange.slot ^ 1})
 
     def hand(m):
-        return send(half_nb.at[m], from_y.at[m], seqs + m, {"tensor": exchange.slot ^ 2})
+        return send(
+            half_nb.at[m + 1], from_y.at[m], seqs + m, {"tensor": exchange.slot ^ 2}
+        )
 
     exchange.greet()
     cross(0).start()
@@ -1069,7 +1147,7 @@
         value = residual[at]
         scale = lax.rsqrt(square_mean(value) + EPS)
         normed = value * scale
-        grad = back_own[at] + back_in[at].astype(F32)
+        grad = back_own[at].astype(F32) + back_in[at].astype(F32)
         grad = grads[at].astype(F32) + scale * (
             grad - normed * jnp.mean(grad * normed, axis=-1, keepdims=True)
         )
@@ -1153,7 +1231,6 @@
         inner(spot)
 
     exchange.send_back(entering)
-    hand(2).start()
     for load in loads[7:]:
         load.wait()
 
@@ -1198,7 +1275,7 @@
     exchange.settle()
     for s in range(seqs):
         cross(s).wait()
-    for m in range(3):
+    for m in range(2):
         hand(m).wait()
 
 
@@ -1212,7 +1289,7 @@
     low = jax.ShapeDtypeStruct((rows, model), BF16)
     return pl.pallas_call(
         functools.partial(retreat_kernel, depth, width, seqs),
-        out_shape=(low,) * 5 + (wide, low, jax.ShapeDtypeStruct(bulk[1].shape, BF16)),
+        out_shape=(low,) * 5 + (wide, low, jax.ShapeDtypeStruct((2,) + bulk[1].shape[1:], BF16)),
         in_specs=[vmem] * (len(early) + len(tables)) + [anywhere] * (len(bulk) + len(late)),
         out_specs=(vmem,) * 6 + (anywhere,) * 2,
         scratch_shapes=[pltpu.VMEM(v.shape, v.dtype) for v in late]
@@ -1225,7 +1302,7 @@
             pltpu.VMEM((rows, model), F32),
         ]
         + state_scratch(heads, seqs, dim, width, depth)
-        + [pltpu.SemaphoreType.DMA((len(late),)), pltpu.SemaphoreType.DMA((2, seqs + 3))],
+        + [pltpu.SemaphoreType.DMA((len(late),)), pltpu.SemaphoreType.DMA((2, seqs + 2))],
         compiler_params=pltpu.CompilerParams(
             collective_id=3, has_side_effects=True, vmem_limit_bytes=60 * 1024 * 1024
         ),
@@ -1251,6 +1328,7 @@
     head_dim = model_width // head_count
     half_dim = head_dim // 2
     row_count = seq_count * group_len
+    core = lax.axis_index("dp")
 
     shard = (w_left.T, w_right.T, w_down)
     grad_own = cotangent.reshape(row_count, model_width)
@@ -1302,17 +1380,9 @@
         depth,
         width,
     )
-    rows_nb = swap(rows_own, "tensor", 1)
-
-    mixed_own, back_own, kept = hidden_part(rows_own, grad_own, shard + (other,), None, F32)
-    mixed_nb, back_nb, kept = hidden_part(rows_nb, grad_nb, shard + (other,), kept, BF16)
-    back_in = swap(back_nb, "tensor", 1)
-    mine, theirs = hidden_grads(kept[1], rows_own, rows_nb, grad_own, grad_nb)
-    moved = swap(theirs, "dp", 1)
-    half_nb = added(mine, moved)
-    mine, theirs = hidden_grads(kept[0], rows_own, rows_nb, grad_own, grad_nb)
-    moved = swap(theirs, "dp", 1)
-
+    mixed, back, half_own, half_nb, back_in, first_y = hidden_part(
+        rows_own, grad_own, grad_nb, shard, other
+    )
     (
         grad_branch,
         grad_ugate_pre,
@@ -1323,9 +1393,9 @@
         mixed_in,
         from_y,
     ) = retreat(
-        (residual, back_own, back_in, grad_own, w_output, merged, ugate),
+        (residual, back, back_in, grad_own, w_output, merged, ugate),
         (rates, powers, cosine, sine_part),
-        (mixed_nb, half_nb),
+        (mixed, half_nb),
         (
             query_low,
             key_low,
@@ -1357,14 +1427,13 @@
         weight_grad(normed_low, grad_ugate_pre),
         weight_grad(gated_low, grad_branch),
     )
-    shard_half = (mine.astype(F32) + moved.astype(F32) + from_y.astype(F32)).astype(BF16)
     hidden = w_down.shape[0]
     sums, hidden_sums = reduce_grads(
-        tuple(g.astype(BF16) for g in partial),
-        shard_half.reshape(3 * hidden, model_width // 2),
-        lax.axis_size("seq"),
-    )
-    mixed_out = (residual + mixed_own + mixed_in.astype(F32)).astype(BF16)
+        tuple(g.astype(BF16) for g in partial), half_own, first_y, from_y, depth
+    )
+    mixed_out = (
+        residual + mixed[:row_count].astype(F32) + mixed_in.astype(F32)
+    ).astype(BF16)
     attention_grads = tuple(
         sums[i * model_width : (i + 1) * model_width].astype(F32) for i in range(len(partial))
     )

time: 379 us -> 341 us (0.90); the launches traced: 375 us -> 341 us
  waiting for transfers between devices: 18.3 us -> 0 us
  local copies, waits for them, and re-layouts: 11.7 us -> 3.54 us
  other arithmetic: 24.8 us -> 20.2 us
    ppermute x4 -> x0, waiting for transfers between devices: 18.3 us -> none  [swap(): lax.ppermute(v, axis, [(i, i ^ bit) for i in range(count)])]
    pallas_call x4 -> x1, Pallas kernels: 44.3 us -> 59.6 us  [hidden_part(): pl.pallas_call(hidden_kernel, out_shape=(two, two, half, half, jax.ShapeD...]
    pallas_call x1, Pallas kernels: 74.6 us -> 62.7 us  [retreat(): pl.pallas_call(functools.partial(retreat_kernel, depth, width, seqs), out...]
    unnamed x41 -> x27, local copies, waits for them, and re-layouts: 9.5 us -> 1.37 us
    convert_element_type x3 -> x1, other arithmetic: 7.45 us -> 3.17 us  [on_device(): mixed_out = (residual + mixed[:row_count].astype(F32) + mixed_in.astype(F...]
  transfers between devices with their start and end apart: 4 -> 0, of which waited for: 2 -> 0; matrix products, arithmetic and copies ran while one was open for 4% -> 0% of each run, Pallas kernels for 26% -> 0%
where the time goes in v1:
time: 341 us
  Pallas kernels  303 us (89%)
  other arithmetic  20.2 us (6%)
  matrix products  13.1 us (4%)
  local copies, waits for them, and re-layouts  3.54 us (1%)
    pallas_call x1, Pallas kernels, reduce_grads(): pl.pallas_call(body, out_shape=(jax.ShapeDtypeStruct((rows, width), BF16)...  119 us
    pallas_call x1, Pallas kernels, retreat(): pl.pallas_call(functools.partial(retreat_kernel, depth, width, seqs), out...  62.7 us
    pallas_call x1, Pallas kernels, attend(): pl.pallas_call(functools.partial(attend_kernel, depth, width, seqs), out_...  62.3 us
    pallas_call x1, Pallas kernels, hidden_part(): pl.pallas_call(hidden_kernel, out_shape=(two, two, half, half, jax.ShapeD...  59.6 us
    dot_general x5, matrix products, weight_grad(): return jnp.einsum('rd,re->de', rows, gradient, preferred_element_type=F32)  13.1 us
    convert_element_type x1, other arithmetic, on_device(): sums[i * model_width:(i + 1) * model_width].astype(F32)  11.1 us

profile of v1, /device:TPU:0, one launch (start us, length us, event | category | flops | bytes accessed | tf_op | source)
XLA Modules:
  0.0 341.1 jit_solution(1608820337864560919)
XLA Ops:
  0.6 1.3 broadcast_in_dim.4.rates
  2.0 0.7 negate_multiply_fusion
  2.6 0.8 broadcast_in_dim.5.powers
  3.5 0.5 fusion
  4.0 0.8 pad_maximum_fusion
  4.9 62.3 %attend.1 = (f32[512,1024]{1,0:T(8,128)}, bf16[512,1024]{1,0:T(8,128)(2,1)}, f32[512,1024]{1,0:T(8,128)}, f32[512,1024]{1,0:T(8,128)}, f32[512,1024]{1,0:T(8,128...) custom-call(bf16[512,1024]{1,0:T(8,128)(2,1)} %bitcast.29, ...), custom_call_target="tpu_custom_call" | custom-call | tf_op jit(solution)/shard_map/attend/pallas_call | solution.py:1005
  67.2 59.6 %hidden_part.1 = (bf16[1024,1024]{1,0:T(8,128)(2,1)}, bf16[1024,1024]{1,0:T(8,128)(2,1)}, bf16[3,704,512]{2,1,0:T(8,128)(2,1)}, bf16[3,704,512]{2,1,0:T(8,128)(2...) custom-call(bf16[512,1024]{1,0:T(8,128)(2,1)} %get-tuple-element.44.rows_own, bf16[512,1024]{1,0:T(8,128)(2,1)} %bitcast.21, ...), custom_call_target="tpu_custom_call" | custom-call | tf_op jit(solution)/shard_map/hidden_part/pallas_call | solution.py:549
  126.8 0.0 copy-start.2
  126.8 62.7 %retreat.1 = (bf16[512,1024]{1,0:T(8,128)(2,1)}, bf16[512,1024]{1,0:T(8,128)(2,1)}, bf16[512,1024]{1,0:T(8,128)(2,1)}, bf16[512,1024]{1,0:T(8,128)(2,1)}, bf16[5...) custom-call(f32[512,1024]{1,0:T(8,128)} %get-tuple-element.43.residual, ...), custom_call_target="tpu_custom_call" | custom-call | tf_op jit(solution)/shard_map/retreat/pallas_call | solution.py:1290
  189.5 0.0 copy-done.2
  189.6 0.0 copy-start.5
  189.6 0.0 copy-start.10
  189.6 3.2 add_convert_fusion
  192.7 0.0 copy-done.5
  192.8 0.0 copy-done.10
  192.8 0.0 copy-start.9
  192.8 2.6 convolution_convert_fusion.4.refs_0_
  195.4 0.0 copy-done.9
  195.4 0.0 copy-start.8
  195.4 2.6 convolution_convert_fusion.3.refs_1_
  198.0 0.0 copy-done.8
  198.0 0.0 copy-start.7
  198.0 2.6 convolution_convert_fusion.2.refs_2_
  200.6 0.0 copy-done.7
  200.6 0.0 copy-start.4
  200.6 0.0 copy-start.6
  200.6 2.6 convolution_convert_fusion.1.refs_3_
  203.3 0.0 copy-done.4
  203.3 0.0 copy-done.6
  203.3 0.0 copy-start
  203.3 0.0 copy-start.1
  203.3 2.6 convolution_convert_fusion.refs_4_
  205.9 0.0 copy-done
  205.9 0.0 copy-done.1
  205.9 118.8 %reduce_grads.1 = (bf16[5120,1024]{1,0:T(8,128)(2,1)}, bf16[2112,1024]{1,0:T(8,128)(2,1)}) custom-call(bf16[1024,1024]{1,0:T(8,128)(2,1)} %convolution_convert_fusion.4.refs_0_, bf16[1024,1024]{1,0:T(8,128)(2,1)} %convolution_convert_fusion.3.refs_1_, bf16[1024,1024]{1,0:T(8,128)(2,1)} %convolution_convert_fusion.2.refs_2_, ...), custom_call_target="tpu_custom_call" | custom-call | tf_op jit(solution)/shard_map/reduce_grads/pallas_call | solution.py:366
  324.8 0.0 slice-start
  324.8 0.0 slice-start.1
  324.8 11.1 %slice_convert_fusion = (f32[1024,1024]{1,0:T(8,128)}, f32[1024,1024]{1,0:T(8,128)}, f32[1024,1024]{1,0:T(8,128)}, f32[1024,1024]{1,0:T(8,128)}, f32[1024,1024]{1,0:T(8,128)}) fusion(bf16[5120,1024]{1,0:T(8,128)(2,1)} %get-tuple-element.74), kind=kLoop, calls=%fused_computation.2 | loop fusion | flops 5242880 | bytes 31457280 | tf_op jit(solution)/shard_map/convert_element_type | solution.py:1438
  335.9 0.0 slice-done
  335.9 0.0 slice-done.1
  335.9 0.0 copy-start.3
  335.9 3.8 %slice_convert_fusion.5 = (f32[704,1024]{1,0:T(8,128)}, f32[1024,704]{0,1:T(8,128)}, f32[1024,704]{0,1:T(8,128)}) fusion(bf16[2112,1024]{1,0:T(8,128)(2,1)S(1)} %bitcast.28), kind=kLoop, calls=%fused_computation.13 | loop fusion | flops 2162688 | bytes 12976128 | tf_op jit(solution)/shard_map/convert_element_type | solution.py:1441
  339.7 0.0 copy-done.3
  339.7 1.3 copy.22
  (4 shorter events, 0.0 us)
Async XLA Ops:
  126.8 62.8 %copy-start.2 = (f32[512,1024]{1,0:T(8,128)S(1)}, f32[512,1024]{1,0:T(8,128)}, u32[]{:S(2)}) copy-start(f32[512,1024]{1,0:T(8,128)} %get-tuple-element.43.residual) | copy-start | bytes 6291460
  189.6 3.2 copy-start.5
  189.6 3.2 copy-start.10
  192.8 2.6 copy-start.9
  195.4 2.6 copy-start.8
  198.0 2.6 copy-start.7
  200.6 2.6 copy-start.4
  200.6 2.6 copy-start.6
  203.3 2.6 copy-start
  203.3 2.6 copy-start.1
  324.8 11.1 %slice-start = ((s8[4325376]{0:T(1024)(128)(4,1)}), s8[4194304]{0:T(1024)(128)(4,1)S(1)}, s32[]{:S(2)}) async-start(s8[4325376]{0:T(1024)(128)(4,1)} %bitcast.27), calls=%async_computation | async-start | bytes 8388608
  324.8 11.1 %slice-start.1 = ((s8[4325376]{0:T(1024)(128)(4,1)}), s8[131072]{0:T(1024)(128)(4,1)S(1)}, s32[]{:S(2)}) async-start(s8[4325376]{0:T(1024)(128)(4,1)} %bitcast.27), calls=%async_computation.1 | async-start | bytes 262144
  335.9 3.9 %copy-start.3 = (f32[512,1024]{1,0:T(8,128)S(1)}, f32[512,1024]{1,0:T(8,128)}, u32[]{:S(2)}) copy-start(f32[512,1024]{1,0:T(8,128)} %get-tuple-element.63) | copy-start | bytes 6291460

commit v2 on v1

--- a/solution.py
+++ b/solution.py
@@ -21,15 +21,20 @@
     return (first.astype(F32) + second.astype(F32)).astype(BF16)
 
 
+RING = 8
+
+
 def reduce_kernel(
     depth,
-    grads,
+    factors,
     pair_own,
     pair_first,
     pair_rest,
     out,
     pair_out,
     pair_in,
+    left_side,
+    right_side,
     own,
     core_in,
     first_in,
@@ -45,7 +50,7 @@
     core = lax.axis_index("dp")
     slot = lax.axis_index("tensor")
     place = lax.axis_index("seq")
-    rows = own.shape[0]
+    rows = out.shape[0]
     chunks = rows // CHUNK
     half, quarter, eighth = CHUNK // 2, CHUNK // 4, CHUNK // 8
     low_side = place < depth // 2
@@ -98,7 +103,7 @@
 
     def to_core(q):
         return remote(
-            own.at[span(base(q) + (1 - core) * half, half)],
+            own.at[q % RING, span((1 - core) * half, half)],
             core_in.at[q],
             sems.at[0],
             q,
@@ -247,20 +252,32 @@
     def pair_core(q):
         return remote(pair.total(q), pair.total(q), pair_sems.at[3], q, {"dp": 1 - core})
 
-    size = rows // len(grads)
+    rights = len(factors) - 2
     loads = [
-        pltpu.make_async_copy(g, own.at[pl.ds(i * size, size)], load_sem.at[i])
-        for i, g in enumerate(grads)
+        pltpu.make_async_copy(g, t, load_sem.at[i])
+        for i, (g, t) in enumerate(
+            zip(
+                factors,
+                [left_side.at[0], left_side.at[1]] + [right_side.at[i] for i in range(rights)],
+            )
+        )
     ]
     for load in loads:
         load.start()
-    per_load = size // CHUNK
-    for i, load in enumerate(loads):
+    for load in loads:
         load.wait()
-
-        @pl.loop(i * per_load, (i + 1) * per_load)
-        def _(q):
-            to_core(q).start()
+    per_matrix = chunks // rights
+
+    def make(q):
+        @pl.when(q >= RING)
+        def _():
+            to_core(q - RING).wait_send()
+
+        m = q // per_matrix
+        columns = pl.ds(pl.multiple_of((q % per_matrix) * CHUNK, CHUNK), CHUNK)
+        own[q % RING] = times_rows(
+            left_side[m // (rights - 1), :, columns], right_side[m]
+        ).astype(BF16)
 
     hidden = pair_first.shape[0]
     for m in range(3):
@@ -270,7 +287,7 @@
     def stage_a(q):
         to_core(q).wait_recv()
         came = core_in.at[q]
-        came[...] = added(own[span(base(q) + core * half, half)], came[...])
+        came[...] = added(own[q % RING, span(core * half, half)], came[...])
 
     def stage_b(q):
         _, _, f, _ = bits(q)
@@ -318,21 +335,23 @@
         pair.step_last(q)
         pair_core(q).start()
 
-    steps = max(pairs + 7 * LAG, pair_chunks + 3 * LAG) + 1
+    steps = max(pairs + 8 * LAG, pair_chunks + 3 * LAG) + 1
 
     @pl.loop(0, steps)
     def _(step):
-        during(step, 7 * LAG, pairs, both(arrived(back_first, back_core)))
-        during(step, 6 * LAG, pairs, both(arrived(back_second, back_first)))
-        during(step, 5 * LAG, pairs, both(last_then_second))
-        during(step, 4 * LAG, pairs, both(line.step_out))
-        during(step, 3 * LAG, pairs, both(line.step_middle))
-        during(step, 2 * LAG, pairs, both(stage_c))
-        during(step, LAG, pairs, both(stage_b))
-        during(step, 0, pairs, both(stage_a))
-        during(step, 2 * LAG, pairs, both(line.step_in))
-        during(step, LAG, pairs, both(start(to_second)))
-        during(step, 0, pairs, both(start(to_first)))
+        during(step, 8 * LAG, pairs, both(arrived(back_first, back_core)))
+        during(step, 7 * LAG, pairs, both(arrived(back_second, back_first)))
+        during(step, 6 * LAG, pairs, both(last_then_second))
+        during(step, 5 * LAG, pairs, both(line.step_out))
+        during(step, 4 * LAG, pairs, both(line.step_middle))
+        during(step, 3 * LAG, pairs, both(stage_c))
+        during(step, 2 * LAG, pairs, both(stage_b))
+        during(step, LAG, pairs, both(stage_a))
+        during(step, 3 * LAG, pairs, both(line.step_in))
+        during(step, 2 * LAG, pairs, both(start(to_second)))
+        during(step, LAG, pairs, both(start(to_first)))
+        during(step, 0, pairs, both(make))
+        during(step, 0, pairs, both(start(to_core)))
         during(step, 3 * LAG, pair_chunks, finish_pair)
         during(step, 2 * LAG, pair_chunks, pair.step_out)
         during(step, LAG, pair_chunks, pair.step_middle)
@@ -341,8 +360,13 @@
     @pl.loop(0, chunks)
     def _(q):
         back_core(q).wait_recv()
-        for copy in (to_core, to_first, to_second, back_second, back_first, back_core):
+        for copy in (to_first, to_second, back_second, back_first, back_core):
             copy(q).wait_send()
+
+        @pl.when(q >= chunks - RING)
+        def _():
+            to_core(q).wait_send()
+
         line.settle(q)
 
     @pl.loop(0, pair_chunks)
@@ -351,9 +375,10 @@
         pair.settle(q)
 
 
-def reduce_grads(grads, half_own, first_y, rest_y, depth):
-    size, width = grads[0].shape
-    rows = size * len(grads)
+def reduce_grads(factors, half_own, first_y, rest_y, depth):
+    count, width = factors[0].shape
+    rights = len(factors) - 2
+    rows = width * rights
     chunks = rows // CHUNK
     pair_chunks = 12
     total_rows, pair_cols = 3 * half_own.shape[1], half_own.shape[2]
@@ -361,7 +386,7 @@
     vmem = pl.BlockSpec(memory_space=pltpu.VMEM)
 
     def body(*refs):
-        reduce_kernel(depth, refs[: len(grads)], *refs[len(grads) :])
+        reduce_kernel(depth, refs[: len(factors)], *refs[len(factors) :])
 
     return pl.pallas_call(
         body,
@@ -369,11 +394,13 @@
             jax.ShapeDtypeStruct((rows, width), BF16),
             jax.ShapeDtypeStruct((total_rows, 2 * pair_cols), BF16),
         ),
-        in_specs=[pl.BlockSpec(memory_space=pl.ANY)] * len(grads) + [vmem] * 3,
+        in_specs=[pl.BlockSpec(memory_space=pl.ANY)] * len(factors) + [vmem] * 3,
         out_specs=(vmem, vmem),
         scratch_shapes=[
             pltpu.VMEM((total_rows, pair_cols), BF16),
-            pltpu.VMEM((rows, width), BF16),
+            pltpu.VMEM((2, count, width), BF16),
+            pltpu.VMEM((rights, count, width), BF16),
+            pltpu.VMEM((RING, CHUNK, width), BF16),
             pltpu.VMEM((chunks, CHUNK // 2, width), BF16),
             pltpu.VMEM((chunks, CHUNK // 4, width), BF16),
             pltpu.VMEM((chunks, CHUNK // 8, width), BF16),
@@ -383,13 +410,13 @@
             pltpu.VMEM((pair_chunks, pair_rows, pair_cols), BF16),
             pltpu.SemaphoreType.DMA((9, 2, chunks)),
             pltpu.SemaphoreType.DMA((4, 2, pair_chunks)),
-            pltpu.SemaphoreType.DMA((len(grads),)),
+            pltpu.SemaphoreType.DMA((len(factors),)),
         ],
         compiler_params=pltpu.CompilerParams(
             collective_id=1, has_side_effects=True, vmem_limit_bytes=50 * 1024 * 1024
         ),
         name="reduce_grads",
-    )(*grads, half_own, first_y, rest_y)
+    )(*factors, half_own, first_y, rest_y)
 
 
 ROWS = 256
@@ -1417,25 +1444,27 @@
         width,
     )
 
-    def weight_grad(rows, gradient):
-        return jnp.einsum("rd,re->de", rows, gradient, preferred_element_type=F32)
-
-    partial = (
-        weight_grad(normed_low, grad_query_pre),
-        weight_grad(normed_low, grad_key_pre),
-        weight_grad(normed_low, grad_value_pre),
-        weight_grad(normed_low, grad_ugate_pre),
-        weight_grad(gated_low, grad_branch),
-    )
     hidden = w_down.shape[0]
     sums, hidden_sums = reduce_grads(
-        tuple(g.astype(BF16) for g in partial), half_own, first_y, from_y, depth
+        (
+            normed_low,
+            gated_low,
+            grad_query_pre,
+            grad_key_pre,
+            grad_value_pre,
+            grad_ugate_pre,
+            grad_branch,
+        ),
+        half_own,
+        first_y,
+        from_y,
+        depth,
     )
     mixed_out = (
         residual + mixed[:row_count].astype(F32) + mixed_in.astype(F32)
     ).astype(BF16)
     attention_grads = tuple(
-        sums[i * model_width : (i + 1) * model_width].astype(F32) for i in range(len(partial))
+        sums[i * model_width : (i + 1) * model_width].astype(F32) for i in range(5)
     )
     left_sum, right_sum, down_sum = (
         hidden_sums[i * hidden : (i + 1) * hidden].astype(F32) for i in range(3)

time: 341 us -> 330 us (0.968)
  matrix products: 13.1 us -> 0 us
    dot_general x5 -> x0, matrix products: 13.1 us -> none  [weight_grad(): return jnp.einsum('rd,re->de', rows, gradient, preferred_element_type=F32)]
where the time goes in v2:
time: 330 us
  Pallas kernels  305 us (92%)
  other arithmetic  20.2 us (6%)
  local copies, waits for them, and re-layouts  3.52 us (1%)
    pallas_call x1, Pallas kernels, reduce_grads(): pl.pallas_call(body, out_shape=(jax.ShapeDtypeStruct((rows, width), BF16)...  121 us
    pallas_call x1, Pallas kernels, retreat(): pl.pallas_call(functools.partial(retreat_kernel, depth, width, seqs), out...  62.7 us
    pallas_call x1, Pallas kernels, attend(): pl.pallas_call(functools.partial(attend_kernel, depth, width, seqs), out_...  62.2 us
    pallas_call x1, Pallas kernels, hidden_part(): pl.pallas_call(hidden_kernel, out_shape=(two, two, half, half, jax.ShapeD...  59.6 us
    convert_element_type x1, other arithmetic, on_device(): sums[i * model_width:(i + 1) * model_width].astype(F32)  11.1 us

profile of v2, /device:TPU:0, one launch (start us, length us, event | category | flops | bytes accessed | tf_op | source)
XLA Modules:
  0.0 329.8 jit_solution(12279484919301660988)
XLA Ops:
  0.6 1.3 broadcast_in_dim.4.rates
  2.0 0.7 negate_multiply_fusion
  2.6 0.8 broadcast_in_dim.5.powers
  3.5 0.5 fusion
  4.0 0.8 pad_maximum_fusion
  4.9 62.2 %attend.1 = (f32[512,1024]{1,0:T(8,128)}, bf16[512,1024]{1,0:T(8,128)(2,1)}, f32[512,1024]{1,0:T(8,128)}, f32[512,1024]{1,0:T(8,128)}, f32[512,1024]{1,0:T(8,128...) custom-call(bf16[512,1024]{1,0:T(8,128)(2,1)} %bitcast.19, ...), custom_call_target="tpu_custom_call" | custom-call | tf_op jit(solution)/shard_map/attend/pallas_call | solution.py:1032
  67.1 59.6 %hidden_part.1 = (bf16[1024,1024]{1,0:T(8,128)(2,1)}, bf16[1024,1024]{1,0:T(8,128)(2,1)}, bf16[3,704,512]{2,1,0:T(8,128)(2,1)}, bf16[3,704,512]{2,1,0:T(8,128)(2...) custom-call(bf16[512,1024]{1,0:T(8,128)(2,1)} %get-tuple-element.44.rows_own, bf16[512,1024]{1,0:T(8,128)(2,1)} %bitcast.11, ...), custom_call_target="tpu_custom_call" | custom-call | tf_op jit(solution)/shard_map/hidden_part/pallas_call | solution.py:576
  126.7 0.0 copy-start.4
  126.7 62.7 %retreat.1 = (bf16[512,1024]{1,0:T(8,128)(2,1)}, bf16[512,1024]{1,0:T(8,128)(2,1)}, bf16[512,1024]{1,0:T(8,128)(2,1)}, bf16[512,1024]{1,0:T(8,128)(2,1)}, bf16[5...) custom-call(f32[512,1024]{1,0:T(8,128)} %get-tuple-element.43.residual, ...), custom_call_target="tpu_custom_call" | custom-call | tf_op jit(solution)/shard_map/retreat/pallas_call | solution.py:1317
  189.4 0.0 copy-done.4
  189.4 0.0 copy-start
  189.4 0.0 copy-start.1
  189.4 0.0 copy-start.2
  189.4 0.0 copy-start.3
  189.4 3.2 add_convert_fusion
  192.6 0.0 copy-done
  192.6 0.0 copy-done.1
  192.6 0.0 copy-done.2
  192.6 0.0 copy-done.3
  192.6 120.8 %reduce_grads.1 = (bf16[5120,1024]{1,0:T(8,128)(2,1)}, bf16[2112,1024]{1,0:T(8,128)(2,1)}) custom-call(bf16[512,1024]{1,0:T(8,128)(2,1)S(1)} %copy-done, bf16[512,1024]{1,0:T(8,128)(2,1)S(1)} %copy-done.1, bf16[512,1024]{1,0:T(8,128)(2,1)S(1)} %copy-done.2, bf16[512,1024]{1,0:T(8,128)(2,1)} %get-tuple-element.67.refs_3_, ...), custom_call_target="tpu_custom_call" | custom-call | tf_op jit(solution)/shard_map/reduce_grads/pallas_call | solution.py:391
  313.4 0.0 slice-start
  313.5 0.0 slice-start.1
  313.5 11.1 %slice_convert_fusion = (f32[1024,1024]{1,0:T(8,128)}, f32[1024,1024]{1,0:T(8,128)}, f32[1024,1024]{1,0:T(8,128)}, f32[1024,1024]{1,0:T(8,128)}, f32[1024,1024]{1,0:T(8,128)}) fusion(bf16[5120,1024]{1,0:T(8,128)(2,1)} %get-tuple-element.74), kind=kLoop, calls=%fused_computation.2 | loop fusion | flops 5242880 | bytes 31457280 | tf_op jit(solution)/shard_map/convert_element_type | solution.py:1467
  324.6 0.0 slice-done
  324.6 0.0 slice-done.1
  324.6 0.0 copy-start.5
  324.6 3.8 %slice_convert_fusion.5 = (f32[704,1024]{1,0:T(8,128)}, f32[1024,704]{0,1:T(8,128)}, f32[1024,704]{0,1:T(8,128)}) fusion(bf16[2112,1024]{1,0:T(8,128)(2,1)S(1)} %bitcast.18), kind=kLoop, calls=%fused_computation.8 | loop fusion | flops 2162688 | bytes 12976128 | tf_op jit(solution)/shard_map/convert_element_type | solution.py:1470
  328.4 0.0 copy-done.5
  328.4 1.3 copy.22
  (4 shorter events, 0.0 us)
Async XLA Ops:
  126.7 62.7 %copy-start.4 = (f32[512,1024]{1,0:T(8,128)S(1)}, f32[512,1024]{1,0:T(8,128)}, u32[]{:S(2)}) copy-start(f32[512,1024]{1,0:T(8,128)} %get-tuple-element.43.residual) | copy-start | bytes 6291460
  189.4 3.2 copy-start
  189.4 3.2 copy-start.1
  189.4 3.2 copy-start.2
  189.4 3.2 copy-start.3
  313.4 11.1 %slice-start = ((s8[4325376]{0:T(1024)(128)(4,1)}), s8[4194304]{0:T(1024)(128)(4,1)S(1)}, s32[]{:S(2)}) async-start(s8[4325376]{0:T(1024)(128)(4,1)} %bitcast.17), calls=%async_computation | async-start | bytes 8388608
  313.5 11.1 %slice-start.1 = ((s8[4325376]{0:T(1024)(128)(4,1)}), s8[131072]{0:T(1024)(128)(4,1)S(1)}, s32[]{:S(2)}) async-start(s8[4325376]{0:T(1024)(128)(4,1)} %bitcast.17), calls=%async_computation.1 | async-start | bytes 262144
  324.6 3.9 %copy-start.5 = (f32[512,1024]{1,0:T(8,128)S(1)}, f32[512,1024]{1,0:T(8,128)}, u32[]{:S(2)}) copy-start(f32[512,1024]{1,0:T(8,128)} %get-tuple-element.63) | copy-start | bytes 6291460

commit v3 on v2

--- a/solution.py
+++ b/solution.py
@@ -512,8 +512,8 @@
     pl.semaphore_wait(barrier, 3)
     for i in range(blocks):
         out_rows(i).start()
-    for load in loads:
-        load.wait()
+    for i in (4, 5, 0, 1, 2):
+        loads[i].wait()
 
     def unit(i, which, weights):
         rows, grads = both[0, span(i)], both[1, span(i)]
@@ -533,7 +533,16 @@
         def _():
             out_rows(i - blocks).wait_recv()
 
+        @pl.when(i == blocks)
+        def _():
+            loads[6].wait()
+
         acc_mixed[...], acc_back[...] = unit(i, 0, own)
+
+        @pl.when(i == 0)
+        def _():
+            loads[3].wait()
+
         more_mixed, more_back = unit(i, 1, other)
         mixed[span(i)] = (acc_mixed[...] + more_mixed).astype(BF16)
         back[span(i)] = (acc_back[...] + more_back).astype(BF16)
@@ -544,19 +553,32 @@
 
     here = pl.ds(pl.multiple_of(core * half, half), half)
     there = pl.ds(pl.multiple_of((1 - core) * half, half), half)
-    for which, out in ((1, half_nb), (0, half_own)):
-
-        @pl.loop(0, 3)
-        def _(m, which=which, out=out):
-            theirs[which, m] = times_rows(kept[which, m], both[m // 2, :, there]).astype(BF16)
-            to_core(which, m).start()
-            out[m] = times_rows(kept[which, m], both[m // 2, :, here]).astype(BF16)
-
-        for m in range(3):
-            to_core(which, m).wait_recv()
-            out[m] = added(out[m], moved[which, m])
-        if which == 1:
-            hand.start()
+
+    def products(which, out, m):
+        theirs[which, m] = times_rows(kept[which, m], both[m // 2, :, there]).astype(BF16)
+        to_core(which, m).start()
+        out[m] = times_rows(kept[which, m], both[m // 2, :, here]).astype(BF16)
+
+    def combine(which, out, m):
+        to_core(which, m).wait_recv()
+        out[m] = added(out[m], moved[which, m])
+
+    products(1, half_nb, 0)
+    combine(1, half_nb, 0)
+    hand.start()
+
+    @pl.loop(1, 3)
+    def _(m):
+        products(1, half_nb, m)
+
+    @pl.loop(0, 3)
+    def _(m):
+        products(0, half_own, m)
+
+    for m in range(1, 3):
+        combine(1, half_nb, m)
+    for m in range(3):
+        combine(0, half_own, m)
     for i in range(blocks):
         out_rows(i).wait_send()
         return_rows(i).wait()
@@ -814,20 +836,12 @@
     residual,
     normed_two,
     attended,
-    query_pre,
-    key_pre,
-    gate,
-    normed_one,
-    query_low,
-    key_low,
-    value_low,
-    query_dec,
-    key_dec,
-    scores_low,
     gated,
     states,
+    early_outs,
     other,
     grads_nb,
+    early,
     w_query,
     w_gate,
     w_output,
@@ -840,7 +854,24 @@
     sems,
     load_sem,
     bulk_sems,
+    store_sem,
 ):
+    (
+        query_pre,
+        key_pre,
+        gate,
+        normed_one,
+        query_low,
+        key_low,
+        value_low,
+        query_dec,
+        key_dec,
+        scores_low,
+    ) = early
+    stores = [
+        pltpu.make_async_copy(a, b, store_sem.at[i])
+        for i, (a, b) in enumerate(zip(early, early_outs))
+    ]
     rows, model = x.shape
     length = rows // seqs
     dim = cosine.shape[1]
@@ -972,15 +1003,17 @@
         inner(spot)
 
     exchange.gather()
-    pass_on(1)
 
     @pl.loop(half, width)
     def _(spot):
         inner(spot)
 
     exchange.send_back(entering)
+    for store in stores:
+        store.start()
+    pass_on(1)
+    pass_on(2)
     pass_last(0)
-    pass_on(2)
     loads[2].wait()
     exchange.arrive()
     pass_last(1)
@@ -1009,6 +1042,8 @@
         value = residual[at]
         normed_two[at] = (value * lax.rsqrt(square_mean(value) + EPS)).astype(BF16)
     pass_last(2)
+    for store in stores:
+        store.wait()
     exchange.settle()
     for m in range(3):
         fetch(m).wait_send()
@@ -1029,22 +1064,46 @@
     wide = jax.ShapeDtypeStruct((rows, model), F32)
     low = jax.ShapeDtypeStruct((rows, model), BF16)
     w_query, w_key, w_value, w_gate, w_output = weights
+    early = (wide,) * 3 + (low,) * 6 + (
+        jax.ShapeDtypeStruct((heads, seqs, length, length), BF16),
+    )
+
+    def body(*refs):
+        at = 14 + 5
+        kept = at + len(early)
+        scratch = kept + 2
+        attend_kernel(
+            depth,
+            width,
+            seqs,
+            *refs[:at],
+            refs[at:kept],
+            *refs[kept:scratch],
+            refs[scratch : scratch + len(early)],
+            *refs[scratch + len(early) :],
+        )
+
     return pl.pallas_call(
-        functools.partial(attend_kernel, depth, width, seqs),
-        out_shape=(wide, low, wide, wide, wide, wide)
-        + (low,) * 6
-        + (
-            jax.ShapeDtypeStruct((heads, seqs, length, length), BF16),
+        body,
+        out_shape=(
+            wide,
+            low,
+            wide,
             low,
             jax.ShapeDtypeStruct((heads, seqs, dim, dim), BF16),
-            jax.ShapeDtypeStruct((3,) + shard[0].shape, BF16),
-            low,
-        ),
+        )
+        + early
+        + (jax.ShapeDtypeStruct((3,) + shard[0].shape, BF16), low),
         in_specs=[vmem] * 3 + [anywhere] * 7 + [vmem] * 4,
-        out_specs=(vmem,) * 15 + (anywhere,) * 2,
-        scratch_shapes=[pltpu.VMEM((model, model), BF16)] * 3
+        out_specs=(vmem,) * 5 + (anywhere,) * (len(early) + 2),
+        scratch_shapes=[pltpu.VMEM(v.shape, v.dtype) for v in early]
+        + [pltpu.VMEM((model, model), BF16)] * 3
         + state_scratch(heads, seqs, dim, width, depth)
-        + [pltpu.SemaphoreType.DMA((3,)), pltpu.SemaphoreType.DMA((2, 12 + seqs))],
+        + [
+            pltpu.SemaphoreType.DMA((3,)),
+            pltpu.SemaphoreType.DMA((2, 12 + seqs)),
+            pltpu.SemaphoreType.DMA((len(early),)),
+        ],
         compiler_params=pltpu.CompilerParams(
             collective_id=2, has_side_effects=True, vmem_limit_bytes=56 * 1024 * 1024
         ),
@@ -1073,9 +1132,6 @@
     back_own,
     back_in,
     grads,
-    w_output,
-    attended,
-    gate,
     rates,
     powers,
     cosine,
@@ -1084,7 +1140,7 @@
     half_nb,
     *rest,
 ):
-    late = rest[:14]
+    late = rest[:17]
     (
         grad_mid_low,
         gate_low,
@@ -1094,9 +1150,12 @@
         grad_tokens,
         mixed_in,
         from_y,
-    ) = rest[14:22]
-    held = rest[22:36]
+    ) = rest[17:25]
+    held = rest[25:42]
     (
+        w_output,
+        attended,
+        gate,
         query_low,
         key_low,
         value_low,
@@ -1128,7 +1187,7 @@
         sems,
         load_sem,
         bulk_sems,
-    ) = rest[36:]
+    ) = rest[42:]
     rows, model = residual.shape
     length = rows // seqs
     dim = cosine.shape[1]
@@ -1153,19 +1212,28 @@
             device_id_type=MESH,
         )
 
-    def cross(s):
-        at = pl.ds(s * length, length)
-        source = mixed_nb.at[pl.ds(rows + s * length, length)]
-        return send(source, mixed_in.at[at], s, {"tensor": exchange.slot ^ 1})
-
-    def hand(m):
+    crosses, hands = 4, 8
+    cross_rows, hand_rows = rows // crosses, 2 * half_nb.shape[1] // hands
+
+    def cross(k):
+        at = pl.ds(k * cross_rows, cross_rows)
+        source = mixed_nb.at[pl.ds(rows + k * cross_rows, cross_rows)]
+        return send(source, mixed_in.at[at], k, {"tensor": exchange.slot ^ 1})
+
+    def hand(k):
+        m, at = k // (hands // 2), pl.ds(k % (hands // 2) * hand_rows, hand_rows)
         return send(
-            half_nb.at[m + 1], from_y.at[m], seqs + m, {"tensor": exchange.slot ^ 2}
-        )
+            half_nb.at[m + 1, at], from_y.at[m, at], crosses + k, {"tensor": exchange.slot ^ 2}
+        )
+
+    def start_bulk(some_crosses, some_hands):
+        for k in some_crosses:
+            cross(k).start()
+        for k in some_hands:
+            hand(k).start()
 
     exchange.greet()
-    cross(0).start()
-    hand(0).start()
+    start_bulk(range(1), range(2))
 
     def spans():
         return [pl.ds(s * length, length) for s in range(seqs)]
@@ -1183,6 +1251,9 @@
 
     def columns_of(spot):
         return pl.ds(pl.multiple_of(spot * tile, tile), tile)
+
+    for load in loads[:3]:
+        load.wait()
 
     @pl.loop(0, width)
     def _(spot):
@@ -1199,7 +1270,7 @@
             scale * (grad - normed * jnp.mean(grad * normed, axis=-1, keepdims=True))
         ).astype(BF16)
 
-    for load in loads[:7]:
+    for load in loads[3:10]:
         load.wait()
 
     @pl.loop(1, width + 1)
@@ -1219,9 +1290,7 @@
             def _(b_static=b_static):
                 exchange.to_peer(b_static).start()
 
-    for s in range(1, seqs):
-        cross(s).start()
-    hand(1).start()
+    start_bulk(range(1, 3), range(2, 5))
 
     def slope(values):
         sigmoid_v = jax.nn.sigmoid(values)
@@ -1258,7 +1327,8 @@
         inner(spot)
 
     exchange.send_back(entering)
-    for load in loads[7:]:
+    start_bulk(range(3, crosses), range(5, hands))
+    for load in loads[10:]:
         load.wait()
 
     @pl.loop(0, width)
@@ -1300,10 +1370,10 @@
             grad - normed * jnp.mean(grad * normed, axis=-1, keepdims=True)
         )
     exchange.settle()
-    for s in range(seqs):
-        cross(s).wait()
-    for m in range(2):
-        hand(m).wait()
+    for k in range(crosses):
+        cross(k).wait()
+    for k in range(hands):
+        hand(k).wait()
 
 
 def retreat(early, tables, bulk, late, seqs, depth, width):
@@ -1329,7 +1399,7 @@
             pltpu.VMEM((rows, model), F32),
         ]
         + state_scratch(heads, seqs, dim, width, depth)
-        + [pltpu.SemaphoreType.DMA((len(late),)), pltpu.SemaphoreType.DMA((2, seqs + 2))],
+        + [pltpu.SemaphoreType.DMA((len(late),)), pltpu.SemaphoreType.DMA((2, 12))],
         compiler_params=pltpu.CompilerParams(
             collective_id=3, has_side_effects=True, vmem_limit_bytes=60 * 1024 * 1024
         ),
@@ -1380,6 +1450,8 @@
         residual,
         rows_own,
         merged,
+        gated_low,
+        state_low,
         query_pre,
         key_pre,
         ugate,
@@ -1390,8 +1462,6 @@
         query_dec,
         key_dec,
         weights_low,
-        gated_low,
-        state_low,
         other,
         grad_nb,
     ) = attend(
@@ -1420,10 +1490,13 @@
         mixed_in,
         from_y,
     ) = retreat(
-        (residual, back, back_in, grad_own, w_output, merged, ugate),
+        (residual, back, back_in, grad_own),
         (rates, powers, cosine, sine_part),
         (mixed, half_nb),
         (
+            w_output,
+            merged,
+            ugate,
             query_low,
             key_low,
             value_low,

time: 330 us -> 316 us (0.958)
  Pallas kernels: 305 us -> 291 us
    pallas_call x1, Pallas kernels: 62.7 us -> 58.3 us  [retreat(): pl.pallas_call(functools.partial(retreat_kernel, depth, width, seqs), out...]
    pallas_call x1, Pallas kernels: 62.2 us -> 57.9 us  [attend(): pl.pallas_call(body, out_shape=(wide, low, wide, low, jax.ShapeDtypeStruc...]
    pallas_call x1, Pallas kernels: 59.6 us -> 55.5 us  [hidden_part(): pl.pallas_call(hidden_kernel, out_shape=(two, two, half, half, jax.ShapeD...]
where the time goes in v3:
time: 316 us; the launch traced here: 315 us
  Pallas kernels  291 us (92%)
  other arithmetic  20.2 us (6%)
  local copies, waits for them, and re-layouts  3.52 us (1%)
    pallas_call x1, Pallas kernels, reduce_grads(): pl.pallas_call(body, out_shape=(jax.ShapeDtypeStruct((rows, width), BF16)...  119 us
    pallas_call x1, Pallas kernels, retreat(): pl.pallas_call(functools.partial(retreat_kernel, depth, width, seqs), out...  58.3 us
    pallas_call x1, Pallas kernels, attend(): pl.pallas_call(body, out_shape=(wide, low, wide, low, jax.ShapeDtypeStruc...  57.9 us
    pallas_call x1, Pallas kernels, hidden_part(): pl.pallas_call(hidden_kernel, out_shape=(two, two, half, half, jax.ShapeD...  55.5 us
    convert_element_type x1, other arithmetic, on_device(): sums[i * model_width:(i + 1) * model_width].astype(F32)  11.1 us

profile of v3, /device:TPU:0, one launch (start us, length us, event | category | flops | bytes accessed | tf_op | source)
XLA Modules:
  0.0 315.5 jit_solution(13703853659283405568)
XLA Ops:
  0.6 1.3 broadcast_in_dim.4.refs_10_.rates
  2.0 0.7 negate_multiply_fusion
  2.6 0.8 broadcast_in_dim.5.refs_11_.powers
  3.5 0.5 fusion
  4.0 0.8 pad_maximum_fusion
  4.9 57.9 %attend.1 = (f32[512,1024]{1,0:T(8,128)}, bf16[512,1024]{1,0:T(8,128)(2,1)}, f32[512,1024]{1,0:T(8,128)}, bf16[512,1024]{1,0:T(8,128)(2,1)}, bf16[8,2,128,128]{3...) custom-call(bf16[512,1024]{1,0:T(8,128)(2,1)} %bitcast.19, ...), custom_call_target="tpu_custom_call" | custom-call | tf_op jit(solution)/shard_map/attend/pallas_call | solution.py:1086
  62.8 55.5 %hidden_part.1 = (bf16[1024,1024]{1,0:T(8,128)(2,1)}, bf16[1024,1024]{1,0:T(8,128)(2,1)}, bf16[3,704,512]{2,1,0:T(8,128)(2,1)}, bf16[3,704,512]{2,1,0:T(8,128)(2...) custom-call(bf16[512,1024]{1,0:T(8,128)(2,1)} %get-tuple-element.44.rows_own, bf16[512,1024]{1,0:T(8,128)(2,1)} %bitcast.11, ...), custom_call_target="tpu_custom_call" | custom-call | tf_op jit(solution)/shard_map/hidden_part/pallas_call | solution.py:598
  118.3 0.0 copy-start.4
  118.4 58.3 %retreat.1 = (bf16[512,1024]{1,0:T(8,128)(2,1)}, bf16[512,1024]{1,0:T(8,128)(2,1)}, bf16[512,1024]{1,0:T(8,128)(2,1)}, bf16[512,1024]{1,0:T(8,128)(2,1)}, bf16[5...) custom-call(f32[512,1024]{1,0:T(8,128)} %get-tuple-element.43.residual, ...), custom_call_target="tpu_custom_call" | custom-call | tf_op jit(solution)/shard_map/retreat/pallas_call | solution.py:1387
  176.6 0.0 copy-done.4
  176.7 0.0 copy-start
  176.7 0.0 copy-start.1
  176.7 0.0 copy-start.2
  176.7 0.0 copy-start.3
  176.7 3.2 %add_convert_fusion = bf16[512,1024]{1,0:T(8,128)(2,1)} fusion(bf16[512,1024]{1,0:T(8,128)(2,1)} %get-tuple-element.62, f32[512,1024]{1,0:T(8,128)S(1)} %copy-done.4, bf16[1024,1024]{1,0:T(8,128)(2,1)} %get-tuple-element.47.mixed_nb), kind=kLoop, calls=%fused_computation.7 | loop fusion | flops 2621440 | bytes 5242880 | tf_op jit(solution)/shard_map/convert_element_type | solution.py:1538
  179.9 0.0 copy-done
  179.9 0.0 copy-done.1
  179.9 0.0 copy-done.2
  179.9 0.0 copy-done.3
  179.9 119.2 %reduce_grads.1 = (bf16[5120,1024]{1,0:T(8,128)(2,1)}, bf16[2112,1024]{1,0:T(8,128)(2,1)}) custom-call(bf16[512,1024]{1,0:T(8,128)(2,1)S(1)} %copy-done.1, bf16[512,1024]{1,0:T(8,128)(2,1)S(1)} %copy-done, bf16[512,1024]{1,0:T(8,128)(2,1)S(1)} %copy-done.2, bf16[512,1024]{1,0:T(8,128)(2,1)} %get-tuple-element.67.refs_3_, ...), custom_call_target="tpu_custom_call" | custom-call | tf_op jit(solution)/shard_map/reduce_grads/pallas_call | solution.py:391
  299.1 0.0 slice-start
  299.2 0.0 slice-start.1
  299.2 11.1 %slice_convert_fusion = (f32[1024,1024]{1,0:T(8,128)}, f32[1024,1024]{1,0:T(8,128)}, f32[1024,1024]{1,0:T(8,128)}, f32[1024,1024]{1,0:T(8,128)}, f32[1024,1024]{1,0:T(8,128)}) fusion(bf16[5120,1024]{1,0:T(8,128)(2,1)} %get-tuple-element.74), kind=kLoop, calls=%fused_computation.2 | loop fusion | flops 5242880 | bytes 31457280 | tf_op jit(solution)/shard_map/convert_element_type | solution.py:1540
  310.3 0.0 slice-done
  310.3 0.0 slice-done.1
  310.3 0.0 copy-start.5
  310.3 3.8 %slice_convert_fusion.5 = (f32[704,1024]{1,0:T(8,128)}, f32[1024,704]{0,1:T(8,128)}, f32[1024,704]{0,1:T(8,128)}) fusion(bf16[2112,1024]{1,0:T(8,128)(2,1)S(1)} %bitcast.18), kind=kLoop, calls=%fused_computation.8 | loop fusion | flops 2162688 | bytes 12976128 | tf_op jit(solution)/shard_map/convert_element_type | solution.py:1543
  314.1 0.0 copy-done.5
  314.1 1.3 copy.22
  (4 shorter events, 0.0 us)
Async XLA Ops:
  118.3 58.3 %copy-start.4 = (f32[512,1024]{1,0:T(8,128)S(1)}, f32[512,1024]{1,0:T(8,128)}, u32[]{:S(2)}) copy-start(f32[512,1024]{1,0:T(8,128)} %get-tuple-element.43.residual) | copy-start | bytes 6291460
  176.7 3.2 %copy-start = (bf16[512,1024]{1,0:T(8,128)(2,1)S(1)}, bf16[512,1024]{1,0:T(8,128)(2,1)}, u32[]{:S(2)}) copy-start(bf16[512,1024]{1,0:T(8,128)(2,1)} %get-tuple-element.65.refs_1_) | copy-start | bytes 3145732
  176.7 3.2 %copy-start.1 = (bf16[512,1024]{1,0:T(8,128)(2,1)S(1)}, bf16[512,1024]{1,0:T(8,128)(2,1)}, u32[]{:S(2)}) copy-start(bf16[512,1024]{1,0:T(8,128)(2,1)} %get-tuple-element.64.refs_0_) | copy-start | bytes 3145732
  176.7 3.2 %copy-start.2 = (bf16[512,1024]{1,0:T(8,128)(2,1)S(1)}, bf16[512,1024]{1,0:T(8,128)(2,1)}, u32[]{:S(2)}) copy-start(bf16[512,1024]{1,0:T(8,128)(2,1)} %get-tuple-element.66.refs_2_) | copy-start | bytes 3145732
  176.7 3.2 %copy-start.3 = (bf16[704,512]{1,0:T(8,128)(2,1)S(1)}, bf16[704,512]{1,0:T(8,128)(2,1)}, u32[]{:S(2)}) copy-start(bf16[704,512]{1,0:T(8,128)(2,1)} %get-tuple-element.72.refs_8_) | copy-start | bytes 2162692
  299.1 11.1 %slice-start = ((s8[4325376]{0:T(1024)(128)(4,1)}), s8[4194304]{0:T(1024)(128)(4,1)S(1)}, s32[]{:S(2)}) async-start(s8[4325376]{0:T(1024)(128)(4,1)} %bitcast.17), calls=%async_computation | async-start | bytes 8388608
  299.2 11.1 %slice-start.1 = ((s8[4325376]{0:T(1024)(128)(4,1)}), s8[131072]{0:T(1024)(128)(4,1)S(1)}, s32[]{:S(2)}) async-start(s8[4325376]{0:T(1024)(128)(4,1)} %bitcast.17), calls=%async_computation.1 | async-start | bytes 262144
  310.3 3.9 %copy-start.5 = (f32[512,1024]{1,0:T(8,128)S(1)}, f32[512,1024]{1,0:T(8,128)}, u32[]{:S(2)}) copy-start(f32[512,1024]{1,0:T(8,128)} %get-tuple-element.63) | copy-start | bytes 6291460

commit v4 on v3

--- a/solution.py
+++ b/solution.py
@@ -30,8 +30,12 @@
     pair_own,
     pair_first,
     pair_rest,
+    residual,
+    mixed_own,
+    mixed_nb,
     out,
     pair_out,
+    mixed_out,
     pair_in,
     left_side,
     right_side,
@@ -46,6 +50,12 @@
     sems,
     pair_sems,
     load_sem,
+    keep_sem,
+    pair_keep_sem,
+    base_part,
+    mixed_part,
+    pair_more,
+    share_sem,
 ):
     core = lax.axis_index("dp")
     slot = lax.axis_index("tensor")
@@ -134,10 +144,15 @@
         _, _, f, g = bits(q)
         return base(q) + core * half + f * quarter + g * eighth
 
+    def keep(q):
+        return pltpu.make_async_copy(
+            line_mid.at[q], out.at[span(block(q), eighth)], keep_sem.at[q]
+        )
+
     def back_second(q):
         _, second, _, _ = bits(q)
         at = span(block(q), eighth)
-        return remote(out.at[at], out.at[at], sems.at[3], q, {"tensor": slot ^ second})
+        return remote(line_mid.at[q], out.at[at], sems.at[3], q, {"tensor": slot ^ second})
 
     def back_first(q):
         first, _, f, _ = bits(q)
@@ -149,8 +164,8 @@
         return remote(out.at[at], out.at[at], sems.at[5], q, {"dp": 1 - core})
 
     class Line:
-        def __init__(self, mine, came, met, total, sem, offset):
-            self.mine, self.came, self.met, self.total = mine, came, met, total
+        def __init__(self, mine, came, met, sem, offset):
+            self.mine, self.came, self.met = mine, came, met
             self.sem, self.offset = sem, offset
 
         def inwards(self, q, source):
@@ -169,7 +184,7 @@
 
         def outwards(self, q):
             return remote(
-                self.total(q), self.total(q), self.sem.at[self.offset + 2], q, {"seq": outward}
+                self.met(q), self.met(q), self.sem.at[self.offset + 2], q, {"seq": outward}
             )
 
         def step_in(self, q):
@@ -196,7 +211,8 @@
             @pl.when(middle)
             def _():
                 self.across(q).wait_recv()
-                self.total(q)[...] = added(self.came(q)[...], self.met(q)[...])
+                met = self.met(q)
+                met[...] = added(self.came(q)[...], met[...])
 
             @pl.when(jnp.logical_not(outermost))
             def _():
@@ -235,7 +251,6 @@
         second_mine,
         lambda q: line_in.at[q],
         lambda q: line_mid.at[q],
-        lambda q: out.at[span(block(q), eighth)],
         sems,
         6,
     )
@@ -244,13 +259,18 @@
         lambda q: pair_in.at[span(q * pair_rows, pair_rows)],
         lambda q: pair_line.at[q],
         lambda q: pair_mid.at[q],
-        lambda q: pair_out.at[span(q * pair_rows, pair_rows), span(core * pair_cols, pair_cols)],
         pair_sems,
         0,
     )
 
+    def pair_block(q):
+        return pair_out.at[span(q * pair_rows, pair_rows), span(core * pair_cols, pair_cols)]
+
+    def pair_keep(q):
+        return pltpu.make_async_copy(pair_mid.at[q], pair_block(q), pair_keep_sem.at[q])
+
     def pair_core(q):
-        return remote(pair.total(q), pair.total(q), pair_sems.at[3], q, {"dp": 1 - core})
+        return remote(pair_mid.at[q], pair_block(q), pair_sems.at[3], q, {"dp": 1 - core})
 
     rights = len(factors) - 2
     loads = [
@@ -262,10 +282,32 @@
             )
         )
     ]
-    for load in loads:
+    tokens = residual.shape[0]
+    parts = [
+        pltpu.make_async_copy(a, b, load_sem.at[len(factors) + i])
+        for i, (a, b) in enumerate(
+            (
+                (residual, base_part),
+                (mixed_own.at[:tokens], mixed_part.at[0]),
+                (mixed_nb, mixed_part.at[1]),
+            )
+        )
+    ]
+    hidden = pair_first.shape[0]
+    thirds = [pl.ds(m * hidden, hidden) for m in range(3)]
+    shares = [
+        pltpu.make_async_copy(pair_own.at[m], pair_in.at[thirds[m]], share_sem.at[0, m])
+        for m in range(3)
+    ] + [
+        pltpu.make_async_copy(
+            pair_first if m == 0 else pair_rest.at[m - 1],
+            pair_more.at[thirds[m]],
+            share_sem.at[1, m],
+        )
+        for m in range(3)
+    ]
+    for load in [loads[0], loads[2]] + shares + [loads[1]] + loads[3:] + parts:
         load.start()
-    for load in loads:
-        load.wait()
     per_matrix = chunks // rights
 
     def make(q):
@@ -279,11 +321,6 @@
             left_side[m // (rights - 1), :, columns], right_side[m]
         ).astype(BF16)
 
-    hidden = pair_first.shape[0]
-    for m in range(3):
-        theirs = pair_first[...] if m == 0 else pair_rest[m - 1]
-        pair_in[pl.ds(m * hidden, hidden)] = added(pair_own[m], theirs)
-
     def stage_a(q):
         to_core(q).wait_recv()
         came = core_in.at[q]
@@ -329,18 +366,26 @@
 
     def last_then_second(q):
         line.step_last(q)
+        keep(q).start()
         back_second(q).start()
+
+    def second_arrived(q):
+        back_second(q).wait_recv()
+        keep(q).wait()
+        back_first(q).start()
 
     def finish_pair(q):
         pair.step_last(q)
+        pair_keep(q).start()
         pair_core(q).start()
 
-    steps = max(pairs + 8 * LAG, pair_chunks + 3 * LAG) + 1
+    late = 2
+    steps = max(pairs + 8 * LAG, pair_chunks + 3 * LAG + late) + 1
 
     @pl.loop(0, steps)
     def _(step):
         during(step, 8 * LAG, pairs, both(arrived(back_first, back_core)))
-        during(step, 7 * LAG, pairs, both(arrived(back_second, back_first)))
+        during(step, 7 * LAG, pairs, both(second_arrived))
         during(step, 6 * LAG, pairs, both(last_then_second))
         during(step, 5 * LAG, pairs, both(line.step_out))
         during(step, 4 * LAG, pairs, both(line.step_middle))
@@ -350,12 +395,38 @@
         during(step, 3 * LAG, pairs, both(line.step_in))
         during(step, 2 * LAG, pairs, both(start(to_second)))
         during(step, LAG, pairs, both(start(to_first)))
+        for m in range(rights):
+
+            @pl.when(step == m * per_matrix // 2)
+            def _(m=m):
+                loads[2 + m].wait()
+                if m == 0:
+                    loads[0].wait()
+                if m == rights - 1:
+                    loads[1].wait()
+
         during(step, 0, pairs, both(make))
         during(step, 0, pairs, both(start(to_core)))
-        during(step, 3 * LAG, pair_chunks, finish_pair)
-        during(step, 2 * LAG, pair_chunks, pair.step_out)
-        during(step, LAG, pair_chunks, pair.step_middle)
-        during(step, 0, pair_chunks, pair.step_in)
+
+        @pl.when(step == 1)
+        def _():
+            for share in shares:
+                share.wait()
+            for at in thirds:
+                pair_in[at] = added(pair_in[at], pair_more[at])
+
+        @pl.when(step == 3)
+        def _():
+            for part in parts:
+                part.wait()
+            mixed_out[...] = (
+                base_part[...] + mixed_part[0].astype(F32) + mixed_part[1].astype(F32)
+            ).astype(BF16)
+
+        during(step, 3 * LAG + late, pair_chunks, finish_pair)
+        during(step, 2 * LAG + late, pair_chunks, pair.step_out)
+        during(step, LAG + late, pair_chunks, pair.step_middle)
+        during(step, late, pair_chunks, pair.step_in)
 
     @pl.loop(0, chunks)
     def _(q):
@@ -372,10 +443,11 @@
     @pl.loop(0, pair_chunks)
     def _(q):
         pair_core(q).wait()
+        pair_keep(q).wait()
         pair.settle(q)
 
 
-def reduce_grads(factors, half_own, first_y, rest_y, depth):
+def reduce_grads(factors, half_own, first_y, rest_y, mixed, depth):
     count, width = factors[0].shape
     rights = len(factors) - 2
     rows = width * rights
@@ -384,6 +456,7 @@
     total_rows, pair_cols = 3 * half_own.shape[1], half_own.shape[2]
     pair_rows = total_rows // pair_chunks
     vmem = pl.BlockSpec(memory_space=pltpu.VMEM)
+    anywhere = pl.BlockSpec(memory_space=pl.ANY)
 
     def body(*refs):
         reduce_kernel(depth, refs[: len(factors)], *refs[len(factors) :])
@@ -393,9 +466,10 @@
         out_shape=(
             jax.ShapeDtypeStruct((rows, width), BF16),
             jax.ShapeDtypeStruct((total_rows, 2 * pair_cols), BF16),
+            jax.ShapeDtypeStruct((count, width), BF16),
         ),
-        in_specs=[pl.BlockSpec(memory_space=pl.ANY)] * len(factors) + [vmem] * 3,
-        out_specs=(vmem, vmem),
+        in_specs=[anywhere] * (len(factors) + 6),
+        out_specs=(anywhere, anywhere, vmem),
         scratch_shapes=[
             pltpu.VMEM((total_rows, pair_cols), BF16),
             pltpu.VMEM((2, count, width), BF16),
@@ -410,13 +484,19 @@
             pltpu.VMEM((pair_chunks, pair_rows, pair_cols), BF16),
             pltpu.SemaphoreType.DMA((9, 2, chunks)),
             pltpu.SemaphoreType.DMA((4, 2, pair_chunks)),
-            pltpu.SemaphoreType.DMA((len(factors),)),
+            pltpu.SemaphoreType.DMA((len(factors) + 3,)),
+            pltpu.SemaphoreType.DMA((chunks,)),
+            pltpu.SemaphoreType.DMA((pair_chunks,)),
+            pltpu.VMEM((count, width), F32),
+            pltpu.VMEM((2, count, width), BF16),
+            pltpu.VMEM((total_rows, pair_cols), BF16),
+            pltpu.SemaphoreType.DMA((2, 3)),
         ],
         compiler_params=pltpu.CompilerParams(
-            collective_id=1, has_side_effects=True, vmem_limit_bytes=50 * 1024 * 1024
+            collective_id=1, has_side_effects=True, vmem_limit_bytes=60 * 1024 * 1024
         ),
         name="reduce_grads",
-    )(*factors, half_own, first_y, rest_y)
+    )(*factors, half_own, first_y, rest_y, *mixed)
 
 
 ROWS = 256
@@ -819,9 +899,9 @@
     depth,
     width,
     seqs,
-    x,
-    w_key,
-    w_value,
+    first_x,
+    first_key,
+    first_value,
     late_query,
     late_gate,
     late_output,
@@ -842,6 +922,9 @@
     other,
     grads_nb,
     early,
+    x,
+    w_key,
+    w_value,
     w_query,
     w_gate,
     w_output,
@@ -879,9 +962,17 @@
     loads = [
         pltpu.make_async_copy(a, b, load_sem.at[i])
         for i, (a, b) in enumerate(
-            ((late_query, w_query), (late_gate, w_gate), (late_output, w_output))
+            (
+                (late_query, w_query),
+                (late_gate, w_gate),
+                (late_output, w_output),
+                (first_x, x),
+                (first_key, w_key),
+                (first_value, w_value),
+            )
         )
     ]
+    loads = loads[3:] + loads[:3]
     for load in loads:
         load.start()
     exchange = States(
@@ -938,12 +1029,15 @@
     fetch(0).start()
     cross(0).start()
     fetch(1).start()
+    loads[0].wait()
     for s in range(seqs):
         at = pl.ds(s * length, length)
         value = x[at].astype(F32)
         normed_one[at] = (value * lax.rsqrt(square_mean(value) + EPS)).astype(BF16)
 
     per_tile = tile // dim
+    loads[1].wait()
+    loads[2].wait()
 
     @pl.loop(1, width + 1)
     def _(step):
@@ -974,8 +1068,8 @@
         cross(s).start()
     fetch(2).start()
     pass_on(0)
-    loads[0].wait()
-    loads[1].wait()
+    loads[3].wait()
+    loads[4].wait()
 
     def inner(spot):
         columns = pl.ds(pl.multiple_of(spot * tile, tile), tile)
@@ -1014,7 +1108,7 @@
     pass_on(1)
     pass_on(2)
     pass_last(0)
-    loads[2].wait()
+    loads[5].wait()
     exchange.arrive()
     pass_last(1)
 
@@ -1094,13 +1188,14 @@
         )
         + early
         + (jax.ShapeDtypeStruct((3,) + shard[0].shape, BF16), low),
-        in_specs=[vmem] * 3 + [anywhere] * 7 + [vmem] * 4,
+        in_specs=[anywhere] * 10 + [vmem] * 4,
         out_specs=(vmem,) * 5 + (anywhere,) * (len(early) + 2),
         scratch_shapes=[pltpu.VMEM(v.shape, v.dtype) for v in early]
-        + [pltpu.VMEM((model, model), BF16)] * 3
+        + [pltpu.VMEM((rows, model), BF16)]
+        + [pltpu.VMEM((model, model), BF16)] * 5
         + state_scratch(heads, seqs, dim, width, depth)
         + [
-            pltpu.SemaphoreType.DMA((3,)),
+            pltpu.SemaphoreType.DMA((6,)),
             pltpu.SemaphoreType.DMA((2, 12 + seqs)),
             pltpu.SemaphoreType.DMA((len(early),)),
         ],
@@ -1518,7 +1613,7 @@
     )
 
     hidden = w_down.shape[0]
-    sums, hidden_sums = reduce_grads(
+    sums, hidden_sums, mixed_out = reduce_grads(
         (
             normed_low,
             gated_low,
@@ -1531,11 +1626,9 @@
         half_own,
         first_y,
         from_y,
+        (residual, mixed, mixed_in),
         depth,
     )
-    mixed_out = (
-        residual + mixed[:row_count].astype(F32) + mixed_in.astype(F32)
-    ).astype(BF16)
     attention_grads = tuple(
         sums[i * model_width : (i + 1) * model_width].astype(F32) for i in range(5)
     )

time: 316 us -> 307 us (0.972)
  Pallas kernels: 291 us -> 283 us
  other arithmetic: 20.2 us -> 17 us
    pallas_call x1, Pallas kernels: 119 us -> 113 us  [reduce_grads(): pl.pallas_call(body, out_shape=(jax.ShapeDtypeStruct((rows, width), BF16)...]
    convert_element_type x1 -> x0, other arithmetic: 3.19 us -> none  [on_device(): mixed_out = (residual + mixed[:row_count].astype(F32) + mixed_in.astype(F...]
where the time goes in v4:
time: 307 us
  Pallas kernels  283 us (92%)
  other arithmetic  17 us (6%)
  local copies, waits for them, and re-layouts  5.46 us (2%)
    pallas_call x1, Pallas kernels, reduce_grads(): pl.pallas_call(body, out_shape=(jax.ShapeDtypeStruct((rows, width), BF16)...  113 us
    pallas_call x1, Pallas kernels, retreat(): pl.pallas_call(functools.partial(retreat_kernel, depth, width, seqs), out...  58.2 us
    pallas_call x1, Pallas kernels, attend(): pl.pallas_call(body, out_shape=(wide, low, wide, low, jax.ShapeDtypeStruc...  56.4 us
    pallas_call x1, Pallas kernels, hidden_part(): pl.pallas_call(hidden_kernel, out_shape=(two, two, half, half, jax.ShapeD...  55.5 us
    convert_element_type x1, other arithmetic, on_device(): sums[i * model_width:(i + 1) * model_width].astype(F32)  11.1 us

profile of v4, /device:TPU:0, one launch (start us, length us, event | category | flops | bytes accessed | tf_op | source)
XLA Modules:
  0.0 306.6 jit_solution(9090945332812859745)
XLA Ops:
  0.6 1.3 broadcast_in_dim.4.refs_10_.rates
  2.0 0.7 negate_multiply_fusion
  2.6 0.8 broadcast_in_dim.5.refs_11_.powers
  3.5 0.5 fusion
  4.0 0.8 pad_maximum_fusion
  4.9 56.4 %attend.1 = (f32[512,1024]{1,0:T(8,128)}, bf16[512,1024]{1,0:T(8,128)(2,1)}, f32[512,1024]{1,0:T(8,128)}, bf16[512,1024]{1,0:T(8,128)(2,1)}, bf16[8,2,128,128]{3...) custom-call(bf16[512,1024]{1,0:T(8,128)(2,1)} %bitcast.19, ...), custom_call_target="tpu_custom_call" | custom-call | tf_op jit(solution)/shard_map/attend/pallas_call | solution.py:1180
  61.2 55.5 %hidden_part.1 = (bf16[1024,1024]{1,0:T(8,128)(2,1)}, bf16[1024,1024]{1,0:T(8,128)(2,1)}, bf16[3,704,512]{2,1,0:T(8,128)(2,1)}, bf16[3,704,512]{2,1,0:T(8,128)(2...) custom-call(bf16[512,1024]{1,0:T(8,128)(2,1)} %get-tuple-element.47.rows_own, bf16[512,1024]{1,0:T(8,128)(2,1)} %bitcast.11, ...), custom_call_target="tpu_custom_call" | custom-call | tf_op jit(solution)/shard_map/hidden_part/pallas_call | solution.py:678
  116.7 58.2 %retreat.1 = (bf16[512,1024]{1,0:T(8,128)(2,1)}, bf16[512,1024]{1,0:T(8,128)(2,1)}, bf16[512,1024]{1,0:T(8,128)(2,1)}, bf16[512,1024]{1,0:T(8,128)(2,1)}, bf16[5...) custom-call(f32[512,1024]{1,0:T(8,128)} %get-tuple-element.46.residual.refs, ...), custom_call_target="tpu_custom_call" | custom-call | tf_op jit(solution)/shard_map/retreat/pallas_call | solution.py:1482
  174.9 113.4 %reduce_grads.1 = (bf16[5120,1024]{1,0:T(8,128)(2,1)}, bf16[2112,1024]{1,0:T(8,128)(2,1)}, bf16[512,1024]{1,0:T(8,128)(2,1)}) custom-call(bf16[512,1024]{1,0:T(8,128)(2,1)} %get-tuple-element.44.refs_0_, bf16[512,1024]{1,0:T(8,128)(2,1)} %get-tuple-element.45.refs_1_, bf16[512,1024]{1,0:T(8,128)(2,1)} %get-tuple-element.65.refs_2_, ...), custom_call_target="tpu_custom_call" | custom-call | tf_op jit(solution)/shard_map/reduce_grads/pallas_call | solution.py:464
  288.3 0.0 slice-start
  288.3 0.0 slice-start.1
  288.4 11.1 %slice_convert_fusion = (f32[1024,1024]{1,0:T(8,128)}, f32[1024,1024]{1,0:T(8,128)}, f32[1024,1024]{1,0:T(8,128)}, f32[1024,1024]{1,0:T(8,128)}, f32[1024,1024]{1,0:T(8,128)}) fusion(bf16[5120,1024]{1,0:T(8,128)(2,1)} %get-tuple-element.76), kind=kLoop, calls=%fused_computation.2 | loop fusion | flops 5242880 | bytes 31457280 | tf_op jit(solution)/shard_map/convert_element_type | solution.py:1633
  299.5 0.0 slice-done
  299.5 0.0 slice-done.1
  299.5 0.0 copy-start.1
  299.5 3.8 %slice_convert_fusion.5 = (f32[704,1024]{1,0:T(8,128)}, f32[1024,704]{0,1:T(8,128)}, f32[1024,704]{0,1:T(8,128)}) fusion(bf16[2112,1024]{1,0:T(8,128)(2,1)S(1)} %bitcast.18), kind=kLoop, calls=%fused_computation.7 | loop fusion | flops 2162688 | bytes 12976128 | tf_op jit(solution)/shard_map/convert_element_type | solution.py:1636
  303.3 0.0 copy-start
  303.3 0.0 copy-done.1
  303.3 1.0 copy.23
  304.3 1.0 copy-done
  305.3 1.3 copy.24
  (4 shorter events, 0.0 us)
Async XLA Ops:
  288.3 11.1 %slice-start = ((s8[4325376]{0:T(1024)(128)(4,1)}), s8[4194304]{0:T(1024)(128)(4,1)S(1)}, s32[]{:S(2)}) async-start(s8[4325376]{0:T(1024)(128)(4,1)} %bitcast.17), calls=%async_computation | async-start | bytes 8388608
  288.3 11.1 %slice-start.1 = ((s8[4325376]{0:T(1024)(128)(4,1)}), s8[131072]{0:T(1024)(128)(4,1)S(1)}, s32[]{:S(2)}) async-start(s8[4325376]{0:T(1024)(128)(4,1)} %bitcast.17), calls=%async_computation.1 | async-start | bytes 262144
  299.5 3.9 %copy-start.1 = (bf16[512,1024]{1,0:T(8,128)(2,1)S(1)}, bf16[512,1024]{1,0:T(8,128)(2,1)}, u32[]{:S(2)}) copy-start(bf16[512,1024]{1,0:T(8,128)(2,1)} %get-tuple-element.74) | copy-start | bytes 3145732
  303.3 2.0 copy-start

commit v5 on v4

--- a/solution.py
+++ b/solution.py
@@ -795,7 +795,7 @@
             def _(j=j):
                 self.to_far(j).start()
 
-    def send_back(self, entering):
+    def send_back(self, entering, between):
         for j in range(1, self.depth):
 
             @pl.when(self.from_far(j))
@@ -806,6 +806,7 @@
             def _(j=j):
                 self.far[j - 1] = jnp.zeros(self.far.shape[1:], BF16)
 
+        between()
         for k in range(self.share):
             head = self.slot * self.share + k
             for s in range(self.local.shape[1]):
@@ -1028,7 +1029,6 @@
     exchange.greet((({"dp": 1 - core}),))
     fetch(0).start()
     cross(0).start()
-    fetch(1).start()
     loads[0].wait()
     for s in range(seqs):
         at = pl.ds(s * length, length)
@@ -1066,6 +1066,7 @@
 
     for s in range(1, seqs):
         cross(s).start()
+    fetch(1).start()
     fetch(2).start()
     pass_on(0)
     loads[3].wait()
@@ -1102,11 +1103,13 @@
     def _(spot):
         inner(spot)
 
-    exchange.send_back(entering)
+    def relays():
+        pass_on(1)
+        pass_on(2)
+
+    exchange.send_back(entering, relays)
     for store in stores:
         store.start()
-    pass_on(1)
-    pass_on(2)
     pass_last(0)
     loads[5].wait()
     exchange.arrive()
@@ -1421,7 +1424,7 @@
     def _(spot):
         inner(spot)
 
-    exchange.send_back(entering)
+    exchange.send_back(entering, lambda: None)
     start_bulk(range(3, crosses), range(5, hands))
     for load in loads[10:]:
         load.wait()

time: 307 us -> 302 us (0.984)
  Pallas kernels: 283 us -> 279 us
where the time goes in v5:
time: 302 us
  Pallas kernels  279 us (92%)
  other arithmetic  17 us (6%)
  local copies, waits for them, and re-layouts  5.46 us (2%)
    pallas_call x1, Pallas kernels, reduce_grads(): pl.pallas_call(body, out_shape=(jax.ShapeDtypeStruct((rows, width), BF16)...  114 us
    pallas_call x1, Pallas kernels, retreat(): pl.pallas_call(functools.partial(retreat_kernel, depth, width, seqs), out...  56.1 us
    pallas_call x1, Pallas kernels, hidden_part(): pl.pallas_call(hidden_kernel, out_shape=(two, two, half, half, jax.ShapeD...  55.5 us
    pallas_call x1, Pallas kernels, attend(): pl.pallas_call(body, out_shape=(wide, low, wide, low, jax.ShapeDtypeStruc...  53.4 us
    convert_element_type x1, other arithmetic, on_device(): sums[i * model_width:(i + 1) * model_width].astype(F32)  11.1 us

profile of v5, /device:TPU:0, one launch (start us, length us, event | category | flops | bytes accessed | tf_op | source)
XLA Modules:
  0.0 302.0 jit_solution(15776900493786630861)
XLA Ops:
  0.6 1.3 broadcast_in_dim.4.refs_10_.rates
  2.0 0.7 negate_multiply_fusion
  2.6 0.8 broadcast_in_dim.5.refs_11_.powers
  3.5 0.5 fusion
  4.0 0.8 pad_maximum_fusion
  4.9 53.4 %attend.1 = (f32[512,1024]{1,0:T(8,128)}, bf16[512,1024]{1,0:T(8,128)(2,1)}, f32[512,1024]{1,0:T(8,128)}, bf16[512,1024]{1,0:T(8,128)(2,1)}, bf16[8,2,128,128]{3...) custom-call(bf16[512,1024]{1,0:T(8,128)(2,1)} %bitcast.19, ...), custom_call_target="tpu_custom_call" | custom-call | tf_op jit(solution)/shard_map/attend/pallas_call | solution.py:1183
  58.3 55.5 %hidden_part.1 = (bf16[1024,1024]{1,0:T(8,128)(2,1)}, bf16[1024,1024]{1,0:T(8,128)(2,1)}, bf16[3,704,512]{2,1,0:T(8,128)(2,1)}, bf16[3,704,512]{2,1,0:T(8,128)(2...) custom-call(bf16[512,1024]{1,0:T(8,128)(2,1)} %get-tuple-element.47.rows_own, bf16[512,1024]{1,0:T(8,128)(2,1)} %bitcast.11, ...), custom_call_target="tpu_custom_call" | custom-call | tf_op jit(solution)/shard_map/hidden_part/pallas_call | solution.py:678
  113.8 56.1 %retreat.1 = (bf16[512,1024]{1,0:T(8,128)(2,1)}, bf16[512,1024]{1,0:T(8,128)(2,1)}, bf16[512,1024]{1,0:T(8,128)(2,1)}, bf16[512,1024]{1,0:T(8,128)(2,1)}, bf16[5...) custom-call(f32[512,1024]{1,0:T(8,128)} %get-tuple-element.46.residual.refs, ...), custom_call_target="tpu_custom_call" | custom-call | tf_op jit(solution)/shard_map/retreat/pallas_call | solution.py:1485
  169.9 113.8 %reduce_grads.1 = (bf16[5120,1024]{1,0:T(8,128)(2,1)}, bf16[2112,1024]{1,0:T(8,128)(2,1)}, bf16[512,1024]{1,0:T(8,128)(2,1)}) custom-call(bf16[512,1024]{1,0:T(8,128)(2,1)} %get-tuple-element.44.refs_0_, bf16[512,1024]{1,0:T(8,128)(2,1)} %get-tuple-element.45.refs_1_, bf16[512,1024]{1,0:T(8,128)(2,1)} %get-tuple-element.65.refs_2_, ...), custom_call_target="tpu_custom_call" | custom-call | tf_op jit(solution)/shard_map/reduce_grads/pallas_call | solution.py:464
  283.7 0.0 slice-start
  283.7 0.0 slice-start.1
  283.8 11.1 %slice_convert_fusion = (f32[1024,1024]{1,0:T(8,128)}, f32[1024,1024]{1,0:T(8,128)}, f32[1024,1024]{1,0:T(8,128)}, f32[1024,1024]{1,0:T(8,128)}, f32[1024,1024]{1,0:T(8,128)}) fusion(bf16[5120,1024]{1,0:T(8,128)(2,1)} %get-tuple-element.76), kind=kLoop, calls=%fused_computation.2 | loop fusion | flops 5242880 | bytes 31457280 | tf_op jit(solution)/shard_map/convert_element_type | solution.py:1636
  294.9 0.0 slice-done
  294.9 0.0 slice-done.1
  294.9 0.0 copy-start.1
  294.9 3.8 %slice_convert_fusion.5 = (f32[704,1024]{1,0:T(8,128)}, f32[1024,704]{0,1:T(8,128)}, f32[1024,704]{0,1:T(8,128)}) fusion(bf16[2112,1024]{1,0:T(8,128)(2,1)S(1)} %bitcast.18), kind=kLoop, calls=%fused_computation.7 | loop fusion | flops 2162688 | bytes 12976128 | tf_op jit(solution)/shard_map/convert_element_type | solution.py:1639
  298.7 0.0 copy-start
  298.7 0.0 copy-done.1
  298.7 1.0 copy.23
  299.7 1.0 copy-done
  300.7 1.3 copy.24
  (4 shorter events, 0.0 us)
Async XLA Ops:
  283.7 11.1 %slice-start = ((s8[4325376]{0:T(1024)(128)(4,1)}), s8[4194304]{0:T(1024)(128)(4,1)S(1)}, s32[]{:S(2)}) async-start(s8[4325376]{0:T(1024)(128)(4,1)} %bitcast.17), calls=%async_computation | async-start | bytes 8388608
  283.7 11.1 %slice-start.1 = ((s8[4325376]{0:T(1024)(128)(4,1)}), s8[131072]{0:T(1024)(128)(4,1)S(1)}, s32[]{:S(2)}) async-start(s8[4325376]{0:T(1024)(128)(4,1)} %bitcast.17), calls=%async_computation.1 | async-start | bytes 262144
  294.9 3.9 %copy-start.1 = (bf16[512,1024]{1,0:T(8,128)(2,1)S(1)}, bf16[512,1024]{1,0:T(8,128)(2,1)}, u32[]{:S(2)}) copy-start(bf16[512,1024]{1,0:T(8,128)(2,1)} %get-tuple-element.74) | copy-start | bytes 3145732
  298.7 2.0 copy-start

commit v6 on v5

--- a/solution.py
+++ b/solution.py
@@ -67,7 +67,7 @@
     outermost = (place == 0) | (place == depth - 1)
     middle = (place == depth // 2 - 1) | (place == depth // 2)
     inward = jnp.where(low_side, place + 1, place - 1)
-    outward = jnp.where(low_side, place - 1, place + 1)
+    outward = jnp.where(outermost, inward, jnp.where(low_side, place - 1, place + 1))
 
     barrier = pltpu.get_barrier_semaphore()
 
@@ -751,7 +751,8 @@
         )
 
     def to_far(self, j):
-        peer = self.place - j if self.backward else self.place + j
+        step = self.depth - j if self.backward else j
+        peer = lax.rem(self.place + step, self.depth)
         return self.copy(self.total, self.far.at[j - 1], self.width + j - 2, {"seq": peer})
 
     def has_far(self, j):

time: 302 us -> 302 us (level)
  no operation moved by 1% of the time
where the time goes in v6:
time: 302 us
  Pallas kernels  279 us (92%)
  other arithmetic  17 us (6%)
  local copies, waits for them, and re-layouts  5.46 us (2%)
    pallas_call x1, Pallas kernels, reduce_grads(): pl.pallas_call(body, out_shape=(jax.ShapeDtypeStruct((rows, width), BF16)...  114 us
    pallas_call x1, Pallas kernels, retreat(): pl.pallas_call(functools.partial(retreat_kernel, depth, width, seqs), out...  56.1 us
    pallas_call x1, Pallas kernels, hidden_part(): pl.pallas_call(hidden_kernel, out_shape=(two, two, half, half, jax.ShapeD...  55.5 us
    pallas_call x1, Pallas kernels, attend(): pl.pallas_call(body, out_shape=(wide, low, wide, low, jax.ShapeDtypeStruc...  53.4 us
    convert_element_type x1, other arithmetic, on_device(): sums[i * model_width:(i + 1) * model_width].astype(F32)  11.1 us

profile of v6, /device:TPU:0, one launch (start us, length us, event | category | flops | bytes accessed | tf_op | source)
XLA Modules:
  0.0 302.0 jit_solution(1463712507171625627)
XLA Ops:
  0.6 1.3 broadcast_in_dim.4.refs_10_.rates
  2.0 0.7 negate_multiply_fusion
  2.6 0.8 broadcast_in_dim.5.refs_11_.powers
  3.5 0.5 fusion
  4.0 0.8 pad_maximum_fusion
  4.9 53.4 %attend.1 = (f32[512,1024]{1,0:T(8,128)}, bf16[512,1024]{1,0:T(8,128)(2,1)}, f32[512,1024]{1,0:T(8,128)}, bf16[512,1024]{1,0:T(8,128)(2,1)}, bf16[8,2,128,128]{3...) custom-call(bf16[512,1024]{1,0:T(8,128)(2,1)} %bitcast.19, ...), custom_call_target="tpu_custom_call" | custom-call | tf_op jit(solution)/shard_map/attend/pallas_call | solution.py:1184
  58.3 55.5 %hidden_part.1 = (bf16[1024,1024]{1,0:T(8,128)(2,1)}, bf16[1024,1024]{1,0:T(8,128)(2,1)}, bf16[3,704,512]{2,1,0:T(8,128)(2,1)}, bf16[3,704,512]{2,1,0:T(8,128)(2...) custom-call(bf16[512,1024]{1,0:T(8,128)(2,1)} %get-tuple-element.47.rows_own, bf16[512,1024]{1,0:T(8,128)(2,1)} %bitcast.11, ...), custom_call_target="tpu_custom_call" | custom-call | tf_op jit(solution)/shard_map/hidden_part/pallas_call | solution.py:678
  113.8 56.1 %retreat.1 = (bf16[512,1024]{1,0:T(8,128)(2,1)}, bf16[512,1024]{1,0:T(8,128)(2,1)}, bf16[512,1024]{1,0:T(8,128)(2,1)}, bf16[512,1024]{1,0:T(8,128)(2,1)}, bf16[5...) custom-call(f32[512,1024]{1,0:T(8,128)} %get-tuple-element.46.residual.refs, ...), custom_call_target="tpu_custom_call" | custom-call | tf_op jit(solution)/shard_map/retreat/pallas_call | solution.py:1486
  169.9 113.8 %reduce_grads.1 = (bf16[5120,1024]{1,0:T(8,128)(2,1)}, bf16[2112,1024]{1,0:T(8,128)(2,1)}, bf16[512,1024]{1,0:T(8,128)(2,1)}) custom-call(bf16[512,1024]{1,0:T(8,128)(2,1)} %get-tuple-element.44.refs_0_, bf16[512,1024]{1,0:T(8,128)(2,1)} %get-tuple-element.45.refs_1_, bf16[512,1024]{1,0:T(8,128)(2,1)} %get-tuple-element.65.refs_2_, ...), custom_call_target="tpu_custom_call" | custom-call | tf_op jit(solution)/shard_map/reduce_grads/pallas_call | solution.py:464
  283.7 0.0 slice-start
  283.7 0.0 slice-start.1
  283.8 11.1 %slice_convert_fusion = (f32[1024,1024]{1,0:T(8,128)}, f32[1024,1024]{1,0:T(8,128)}, f32[1024,1024]{1,0:T(8,128)}, f32[1024,1024]{1,0:T(8,128)}, f32[1024,1024]{1,0:T(8,128)}) fusion(bf16[5120,1024]{1,0:T(8,128)(2,1)} %get-tuple-element.76), kind=kLoop, calls=%fused_computation.2 | loop fusion | flops 5242880 | bytes 31457280 | tf_op jit(solution)/shard_map/convert_element_type | solution.py:1637
  294.9 0.0 slice-done
  294.9 0.0 slice-done.1
  294.9 0.0 copy-start.1
  294.9 3.8 %slice_convert_fusion.5 = (f32[704,1024]{1,0:T(8,128)}, f32[1024,704]{0,1:T(8,128)}, f32[1024,704]{0,1:T(8,128)}) fusion(bf16[2112,1024]{1,0:T(8,128)(2,1)S(1)} %bitcast.18), kind=kLoop, calls=%fused_computation.7 | loop fusion | flops 2162688 | bytes 12976128 | tf_op jit(solution)/shard_map/convert_element_type | solution.py:1640
  298.7 0.0 copy-start
  298.7 0.0 copy-done.1
  298.7 1.0 copy.23
  299.7 1.0 copy-done
  300.7 1.3 copy.24
  (4 shorter events, 0.0 us)
Async XLA Ops:
  283.7 11.1 %slice-start = ((s8[4325376]{0:T(1024)(128)(4,1)}), s8[4194304]{0:T(1024)(128)(4,1)S(1)}, s32[]{:S(2)}) async-start(s8[4325376]{0:T(1024)(128)(4,1)} %bitcast.17), calls=%async_computation | async-start | bytes 8388608
  283.7 11.1 %slice-start.1 = ((s8[4325376]{0:T(1024)(128)(4,1)}), s8[131072]{0:T(1024)(128)(4,1)S(1)}, s32[]{:S(2)}) async-start(s8[4325376]{0:T(1024)(128)(4,1)} %bitcast.17), calls=%async_computation.1 | async-start | bytes 262144
  294.9 3.9 %copy-start.1 = (bf16[512,1024]{1,0:T(8,128)(2,1)S(1)}, bf16[512,1024]{1,0:T(8,128)(2,1)}, u32[]{:S(2)}) copy-start(bf16[512,1024]{1,0:T(8,128)(2,1)} %get-tuple-element.74) | copy-start | bytes 3145732
  298.7 2.0 copy-start
